TPU v7x, 512 devices: a whole 4x8x8 slice. The times are simulated.
512 devices in a mesh: gx: 32 (over x_lo, z, core), yz: 16 (over x_hi, y).
Axes of the slice: x: 4 (x_hi: 2, x_lo: 2; x = x_hi * 2 + x_lo), y: 8, z: 8, core: 2. Of those that a mesh axis runs over, the one named last changes fastest.
Arguments:
- leaf_moments: bfloat16 [256, 128, 256], P('gx', 'yz'), may hold values from -6 to 6
- leaf_list: int32 [256, 128, 16], P('gx', 'yz'), may hold values from 0 to 288
- leaf_op: int32 [256, 128, 16], P('gx', 'yz'), may hold values from 0 to 15
- leaf_parent: int32 [256, 128], P('gx', 'yz'), may hold values from 0 to 127, as said below
- leaf_octant: int32 [256, 128], P('gx', 'yz'), may hold values from 0 to 7, as said below
- parent_list: int32 [32, 128, 8], P('gx', 'yz'), may hold values from 0 to 639
- parent_op: int32 [32, 128, 8], P('gx', 'yz'), may hold values from 0 to 15
- operators: bfloat16 [16, 256, 256], replicated, may hold values from -0.09375 to 0.09375
- shift_up: bfloat16 [8, 256, 256], replicated, may hold values from -0.125 to 0.125
- density: bfloat16 [8192, 128, 128], P(('gx', 'yz')), may hold values from -6 to 6
- nearby_coulomb_kernel: bfloat16 [8, 128, 128], replicated, may hold values from -0.1875 to 0.1875
- near_src: int32 [8192, 16], P(('gx', 'yz')), may hold values from 0 to 15
- near_kind: int32 [8192, 16], P(('gx', 'yz')), may hold values from 0 to 7
- near_count: int32 [8192], P(('gx', 'yz')), may hold values from 1 to 16
- eval_rows: float32 [128, 16], replicated, may hold values from -1.5 to 1.5
- eval_cols: float32 [16, 128], replicated, may hold values from -1.5 to 1.5
Outputs:
- coulomb: bfloat16 [8192, 128, 128], P(('gx', 'yz'))
Inputs may be any that keep to these rules, and one draw needn't show every extreme that they name: `leaf_parent`: within each column of leaf blocks (a // 8 fixed) every coarse box number is named by exactly 8 leaves. `leaf_octant`: the 8 leaves of one coarse box have 8 different octants.
All inputs are finite; a program needn't handle non-finite values.
Results may differ from a plain program's by a relative error of at most 0.0026.
Values may be sent and summed in bfloat16 or wider, within the bound.
No kernel may reach another device: no remote copies, remote signals or barrier semaphores. Data moves between devices by JAX's collectives and lax.ppermute only.
A program may use at most 64 MiB of HBM per device.

v0:
```python
import jax
import jax.numpy as jnp
from jax import lax
from jax.sharding import PartitionSpec as P


def extended(value, sides, width):
    for axis, dim in sides:
        peers, length = (lax.axis_size(axis), value.shape[dim])
        up = [(i, (i + 1) % peers) for i in range(peers)]
        down = [(j, i) for i, j in up]
        last = lax.slice_in_dim(value, length - width, length, axis=dim)
        leading = lax.slice_in_dim(value, 0, width, axis=dim)
        before = lax.ppermute(last, axis, up)
        after = lax.ppermute(leading, axis, down)
        value = jnp.concatenate([before, value, after], axis=dim)
    return value


def in_blocks(value, dim, peers):
    before, after = (value.shape[:dim], value.shape[dim + 1 :])
    return jnp.moveaxis(value.reshape(*before, peers, -1, *after), dim, 0)


def sum_at_owner(value, axis, dim):
    tiles = in_blocks(value, dim, lax.axis_size(axis))
    arrived = lax.all_to_all(tiles, axis, split_axis=0, concat_axis=0, tiled=True)
    return arrived.sum(axis=0)


def shifted_2(block, axis, distance):
    devices = range(lax.axis_size(axis))
    route = [((i - distance) % len(devices), i) for i in devices]
    return lax.ppermute(block, axis, route)


def laid_out(tiles, dim):
    tiles = jnp.moveaxis(tiles, 0, dim)
    shape = tiles.shape
    return tiles.reshape(*shape[:dim], shape[dim] * shape[dim + 1], *shape[dim + 2 :])


def sent_to_all(value, axis):
    copies = jnp.broadcast_to(value, (lax.axis_size(axis), *value.shape))
    return lax.all_to_all(copies, axis, split_axis=0, concat_axis=0, tiled=True)


def gather_directly(value, axis, dim):
    return laid_out(sent_to_all(value, axis), dim)


def expand_rows(values, labels, groups):
    chosen = labels[:, None] == jnp.arange(groups, dtype=jnp.int32)[None, :]
    return jnp.where(chosen[:, :, None], values[:, None, :], jnp.zeros((), values.dtype))


def listed_sum(flat_window, slot_codes, op_index, operators):
    ops_count = operators.shape[0]
    coeffs = operators.shape[1]
    stacked = operators.reshape(ops_count * coeffs, coeffs)
    targets = slot_codes.shape[0]

    def add_slot(slot_number, summed):
        picked = jnp.take(flat_window, slot_codes[:, slot_number], axis=0)
        spread = expand_rows(picked, op_index[:, slot_number], ops_count).reshape(
            targets, ops_count * coeffs
        )
        return summed + jnp.dot(spread, stacked, preferred_element_type=jnp.float32)

    return lax.fori_loop(
        0, slot_codes.shape[1], add_slot, jnp.zeros((targets, coeffs), jnp.float32)
    )


def body(
    leaf_moments,
    leaf_list,
    leaf_op,
    leaf_parent,
    leaf_octant,
    parent_list,
    parent_op,
    operators,
    shift_up,
    density,
    nearby_coulomb_kernel,
    near_src,
    near_kind,
    near_count,
    eval_rows,
    eval_cols,
):
    leaf_side = leaf_moments.shape[0]
    coeffs = leaf_moments.shape[2]
    leaves = leaf_side * leaf_side
    code_span = 2 * leaf_side + 1
    window = extended(leaf_moments, (("gx", 0), ("yz", 1)), leaf_side)
    flat_window = window.reshape(9 * leaves, coeffs)
    index_first = lax.broadcasted_iota(jnp.int32, leaf_list.shape, 0)
    index_second = lax.broadcasted_iota(jnp.int32, leaf_list.shape, 1)
    window_codes = (
        (index_first + leaf_list // code_span) * (3 * leaf_side)
        + index_second
        + leaf_list % code_span
    )
    far_local = listed_sum(
        flat_window, window_codes.reshape(leaves, -1), leaf_op.reshape(leaves, -1), operators
    )
    parents_of = leaf_parent.reshape(leaves)
    octants = leaf_octant.reshape(leaves)
    child_spread = expand_rows(leaf_moments.reshape(leaves, coeffs), octants, 8)
    translated = jnp.einsum(
        "lop,opq->lq", child_spread, shift_up, preferred_element_type=jnp.float32
    )
    per_device = parent_list.shape[1]
    column_count = per_device * lax.axis_size("yz")
    owner_table = (
        jnp.arange(column_count, dtype=jnp.int32)[:, None] == parents_of[None, :]
    ).astype(jnp.float32)
    own_moments = sum_at_owner(
        jnp.dot(owner_table, translated, precision=lax.Precision.HIGHEST), "yz", 0
    ).astype(jnp.bfloat16)
    shifted = [
        shifted_2(own_moments, "gx", index_displacement) for index_displacement in (2, 1, -1, -2)
    ]
    own_window = jnp.stack([shifted[0], shifted[1], own_moments, shifted[2], shifted[3]])
    parent_window = gather_directly(own_window, "yz", 1).reshape(5 * column_count, coeffs)
    own_locals = listed_sum(parent_window, parent_list[0], parent_op[0], operators).astype(
        jnp.bfloat16
    )
    column_locals = gather_directly(own_locals, "yz", 0)
    parent_rows = jnp.take(column_locals, parents_of, axis=0)
    lowered = jnp.einsum(
        "lop,oqp->lq",
        expand_rows(parent_rows, octants, 8),
        shift_up,
        preferred_element_type=jnp.float32,
    )
    leaf_local = far_local + lowered
    tiles_dev = density.shape[0]
    box_tile = leaves // tiles_dev
    shell_side = eval_rows.shape[0]
    harmonics = eval_rows.shape[1]
    blocks = leaf_local.reshape(tiles_dev, box_tile, harmonics, harmonics)
    left_half = jnp.einsum(
        "rai,trij->traj",
        eval_rows.reshape(box_tile, shell_side // box_tile, harmonics),
        blocks,
        precision=lax.Precision.HIGHEST,
    )
    left_half = left_half.reshape(tiles_dev, shell_side, harmonics)
    far_tiles = jnp.einsum("taj,jb->tab", left_half, eval_cols, precision=lax.Precision.HIGHEST)
    kinds_count = nearby_coulomb_kernel.shape[0]
    slot_live = jnp.arange(near_src.shape[1], dtype=jnp.int32)[None, :] < near_count[:, None]
    partner_hits = near_src[:, :, None] == jnp.arange(tiles_dev, dtype=jnp.int32)[None, None, :]
    flat_density = density.reshape(tiles_dev, shell_side * shell_side)
    nearby_tile_list = jnp.zeros((tiles_dev, shell_side, shell_side), jnp.float32)
    for interaction_kind in range(kinds_count):
        taken = slot_live & (near_kind == interaction_kind)
        selection = jnp.sum((taken[:, :, None] & partner_hits).astype(jnp.int32), axis=1).astype(
            jnp.bfloat16
        )
        collected_tiles = jnp.dot(
            selection, flat_density, preferred_element_type=jnp.float32
        ).reshape(tiles_dev, shell_side, shell_side)
        kernel_wide = nearby_coulomb_kernel[interaction_kind].astype(jnp.float32)
        nearby_tile_list = nearby_tile_list + jnp.einsum(
            "zf,pfo->pzo", kernel_wide, collected_tiles, precision=lax.Precision.HIGHEST
        )
    return (nearby_tile_list + far_tiles).astype(jnp.bfloat16)


def solution(mesh):
    in_specs = (
        P("gx", "yz", None),
        P("gx", "yz", None),
        P("gx", "yz", None),
        P("gx", "yz"),
        P("gx", "yz"),
        P("gx", "yz", None),
        P("gx", "yz", None),
        P(),
        P(),
        P(("gx", "yz"), None, None),
        P(),
        P(("gx", "yz"), None),
        P(("gx", "yz"), None),
        P(("gx", "yz")),
        P(),
        P(),
    )
    out_specs = P(("gx", "yz"), None, None)
    return jax.shard_map(body, mesh=mesh, in_specs=in_specs, out_specs=out_specs, check_vma=False)
```

profile of v0, /device:TPU:4, one launch (start us, length us, event | category | flops | bytes accessed | tf_op | source)
XLA Modules:
  0.0 193.7 jit_solution(15741559765922614859)
XLA Ops:
  0.0 2.0 %collective-permute-start = (bf16[8,8,256]{2,1,0:T(8,128)(2,1)}, bf16[8,8,256]{2,1,0:T(8,128)(2,1)S(1)}, u32[]{:S(2)}, u32[]{:S(2)}) collective-permute-start(bf16[8,8,256]{2,1,0:T(8,128)(2,1)} %param.20), channel_id=1, source_target_pairs={{0,16},{16,32},{32,48},{48,64},{64,80},{80,96},{96,112},{112,128},... | collective-permute-start | bytes 98312 | tf_op jit(solution)/shard_map/ppermute | solution.py:14
  2.1 11.0 %collective-permute-start.1 = (bf16[8,8,256]{2,1,0:T(8,128)(2,1)}, bf16[8,8,256]{2,1,0:T(8,128)(2,1)S(1)}, u32[]{:S(2)}, u32[]{:S(2)}) collective-permute-start(bf16[8,8,256]{2,1,0:T(8,128)(2,1)} %param.20), channel_id=1, source_target_pairs={{16,0},{32,16},{48,32},{64,48},{80,64},{96,80},{112,96},{128,112},... | collective-permute-start | bytes 98312 | tf_op jit(solution)/shard_map/ppermute | solution.py:15
  16.6 10.1 %all-to-all-start = ((f32[16,8,256]{2,1,0:T(8,128)}), f32[16,8,256]{2,1,0:T(8,128)S(1)}, u32[]{:S(2)}, u32[]{:S(2)}) async-start(f32[16,8,256]{2,1,0:T(8,128)} %convolution_bitcast_fusion.1), calls=%async_computation | async-start | bytes 262144 | tf_op jit(solution)/shard_map/all_to_all | solution.py:27
  27.5 1.2 convert_reduce_fusion
  33.1 1.1 convolution_add_fusion.9
  35.3 1.1 convolution_add_fusion.7
  36.4 1.1 convolution_add_fusion.6
  37.5 1.1 convolution_add_fusion.5
  38.6 1.1 convolution_add_fusion.4
  39.8 2.3 %fusion = f32[16,128,128]{1,2,0:T(8,128)} fusion(f32[16,128,128]{2,1,0:T(8,128)S(1)} %convolution_add_fusion.4, f32[16,128,128]{2,0,1:T(8,128)S(1)} %fusion.12, bf16[8,128,128]{2,1,0:T(8,128)(2,1)S(1)} %copy-done.4), kind=kOutput, calls=%fused_computation.21 | convolution fusion | flops 402915328 | bytes 3178496 | tf_op jit(solution)/shard_map/zf,pfo->pzo/dot_general | solution.py:167
  42.1 2.1 %collective-permute-start.4 = (bf16[8,256]{1,0:T(8,128)(2,1)S(1)}, bf16[8,256]{1,0:T(8,128)(2,1)S(1)}, u32[]{:S(2)}, u32[]{:S(2)}) collective-permute-start(bf16[8,256]{1,0:T(8,128)(2,1)S(1)} %reduce_sum.89), channel_id=1, source_target_pairs={{480,0},{496,16},{0,32},{16,48},{32,64},{48,80},{64,96},{80,112},{... | collective-permute-start | bytes 12296 | tf_op jit(solution)/shard_map/ppermute | solution.py:34
  44.8 1.9 collective-permute-start.5
  46.8 5.8 %collective-permute-start.6 = (bf16[8,256]{1,0:T(8,128)(2,1)S(1)}, bf16[8,256]{1,0:T(8,128)(2,1)S(1)}, u32[]{:S(2)}, u32[]{:S(2)}) collective-permute-start(bf16[8,256]{1,0:T(8,128)(2,1)S(1)} %reduce_sum.89), channel_id=1, source_target_pairs={{16,0},{32,16},{48,32},{64,48},{80,64},{96,80},{112,96},{128,112},... | collective-permute-start | bytes 12296 | tf_op jit(solution)/shard_map/ppermute | solution.py:34
  52.5 3.9 %collective-permute-start.7 = (bf16[8,256]{1,0:T(8,128)(2,1)S(1)}, bf16[8,256]{1,0:T(8,128)(2,1)S(1)}, u32[]{:S(2)}, u32[]{:S(2)}) collective-permute-start(bf16[8,256]{1,0:T(8,128)(2,1)S(1)} %reduce_sum.89), channel_id=1, source_target_pairs={{32,0},{48,16},{64,32},{80,48},{96,64},{112,80},{128,96},{144,112}... | collective-permute-start | bytes 12296 | tf_op jit(solution)/shard_map/ppermute | solution.py:34
  56.5 1.5 collective-permute-done.7
  58.8 9.6 %all-to-all-start.1 = ((bf16[16,5,8,256]{3,2,1,0:T(8,128)(2,1)}), bf16[16,5,8,256]{3,2,1,0:T(8,128)(2,1)}, u32[]{:S(2)}, u32[]{:S(2)}) async-start(bf16[16,5,8,256]{3,2,1,0:T(8,128)(2,1)} %broadcast_in_dim.208), calls=%async_computation.1 | async-start | bytes 655360 | tf_op jit(solution)/shard_map/all_to_all | solution.py:45
  69.5 4.6 %collective-permute-start.3 = (bf16[24,8,256]{2,1,0:T(8,128)(2,1)S(1)}, bf16[24,8,256]{2,1,0:T(8,128)(2,1)S(1)}, u32[]{:S(2)}, u32[]{:S(2)}) collective-permute-start(bf16[24,8,256]{2,1,0:T(8,128)(2,1)S(1)} %constant_dynamic-update-slice_fusion), channel_id=1, source_target_pairs={{1,0},{2,1},{3,2},{4,3},{5,4},{6,5},{7,6},{8,7},{9,8},{10,9},{11,1... | collective-permute-start | bytes 294920 | tf_op jit(solution)/shard_map/ppermute | solution.py:15
  74.1 1.9 collective-permute-start.2
  76.9 7.3 %collective-permute-done.2 = bf16[24,8,256]{2,1,0:T(8,128)(2,1)S(1)} collective-permute-done((bf16[24,8,256]{2,1,0:T(8,128)(2,1)S(1)}, bf16[24,8,256]{2,1,0:T(8,128)(2,1)S(1)}, u32[]{:S(2)}, u32[]{:S(2)}) %collective-permute-start.2) | collective-permute-done | bytes 98336 | tf_op jit(solution)/shard_map/ppermute | solution.py:14
  84.2 1.7 copy.95
  86.0 18.3 %while.29 = (s32[]{:T(128)}, f32[8,256]{1,0:T(8,128)S(1)}, s32[8,8]{0,1:T(8,128)S(1)}, s32[8,8]{0,1:T(8,128)S(1)}, bf16[640,256]{1,0:T(8,128)(2,1)}, /*index=5*/bf16[4096,256]{1,0:T(8,128)(2,1)S(1)}, s32[]{:T(128)}, s32[]{:T(128)}) while((s32[]{:T(128)}, f32[8,256]{1,0:T(8,128)S(1)}, s32[8,8]{0,1:T(8,128)S(1)}, ...), condition=%wide.region_12.13_spmd.clone, body=%wide.region_11.12_spmd.clone.sunk | while | flops 16817332 | bytes 2400863 | solution.py:70
  86.1 1.6 gather_fusion.1
  88.4 1.6 gather_fusion.1
  90.6 1.6 gather_fusion.1
  92.9 1.6 gather_fusion.1
  95.2 1.6 gather_fusion.1
  97.5 1.6 gather_fusion.1
  99.8 1.6 gather_fusion.1
  102.1 1.6 gather_fusion.1
  104.9 6.3 %all-to-all-start.2 = ((bf16[16,8,256]{2,1,0:T(8,128)(2,1)}), bf16[16,8,256]{2,1,0:T(8,128)(2,1)S(1)}, u32[]{:S(2)}, u32[]{:S(2)}) async-start(bf16[16,8,256]{2,1,0:T(8,128)(2,1)} %broadcast_in_dim.209), calls=%async_computation.2 | async-start | bytes 131072 | tf_op jit(solution)/shard_map/all_to_all | solution.py:45
  111.2 75.6 %while.28 = (s32[]{:T(128)}, f32[64,256]{1,0:T(8,128)}, s32[64,16]{0,1:T(8,128)S(1)}, s32[64,16]{0,1:T(8,128)S(1)}, bf16[576,256]{1,0:T(8,128)(2,1)S(1)}, /*inde...) while((s32[]{:T(128)}, f32[64,256]{1,0:T(8,128)}, s32[64,16]{0,1:T(8,128)S(1)}, ...), condition=%wide.region_9.10_spmd.clone, body=%wide.region_8.9_spmd.clone.sunk | while | flops 134531456 | bytes 4563039 | solution.py:70
  113.8 2.1 %convolution_add_fusion.12 = f32[64,256]{1,0:T(8,128)} fusion(bf16[64,4096]{1,0:T(8,128)(2,1)} %bitcast.208, bf16[4096,256]{1,0:T(8,128)(2,1)S(1)} %get-tuple-element.468, f32[64,256]{1,0:T(8,128)} %get-tuple-element.456, pred[]{:T(512)S(6)} %compare.6), kind=kOutput, calls=%fused_computation.3.clone.1 | convolution fusion | flops 134250496 | bytes 2752513 | tf_op jit(solution)/shard_map/while/body/eval_jaxpr/dot_general | solution.py:68
  118.5 2.1 %convolution_add_fusion.12 = f32[64,256]{1,0:T(8,128)} fusion(bf16[64,4096]{1,0:T(8,128)(2,1)} %bitcast.208, bf16[4096,256]{1,0:T(8,128)(2,1)S(1)} %get-tuple-element.468, f32[64,256]{1,0:T(8,128)} %get-tuple-element.456, pred[]{:T(512)S(6)} %compare.6), kind=kOutput, calls=%fused_computation.3.clone.1 | convolution fusion | flops 134250496 | bytes 2752513 | tf_op jit(solution)/shard_map/while/body/eval_jaxpr/dot_general | solution.py:68
  123.2 2.1 %convolution_add_fusion.12 = f32[64,256]{1,0:T(8,128)} fusion(bf16[64,4096]{1,0:T(8,128)(2,1)} %bitcast.208, bf16[4096,256]{1,0:T(8,128)(2,1)S(1)} %get-tuple-element.468, f32[64,256]{1,0:T(8,128)} %get-tuple-element.456, pred[]{:T(512)S(6)} %compare.6), kind=kOutput, calls=%fused_computation.3.clone.1 | convolution fusion | flops 134250496 | bytes 2752513 | tf_op jit(solution)/shard_map/while/body/eval_jaxpr/dot_general | solution.py:68
  128.0 2.1 %convolution_add_fusion.12 = f32[64,256]{1,0:T(8,128)} fusion(bf16[64,4096]{1,0:T(8,128)(2,1)} %bitcast.208, bf16[4096,256]{1,0:T(8,128)(2,1)S(1)} %get-tuple-element.468, f32[64,256]{1,0:T(8,128)} %get-tuple-element.456, pred[]{:T(512)S(6)} %compare.6), kind=kOutput, calls=%fused_computation.3.clone.1 | convolution fusion | flops 134250496 | bytes 2752513 | tf_op jit(solution)/shard_map/while/body/eval_jaxpr/dot_general | solution.py:68
  132.7 2.1 %convolution_add_fusion.12 = f32[64,256]{1,0:T(8,128)} fusion(bf16[64,4096]{1,0:T(8,128)(2,1)} %bitcast.208, bf16[4096,256]{1,0:T(8,128)(2,1)S(1)} %get-tuple-element.468, f32[64,256]{1,0:T(8,128)} %get-tuple-element.456, pred[]{:T(512)S(6)} %compare.6), kind=kOutput, calls=%fused_computation.3.clone.1 | convolution fusion | flops 134250496 | bytes 2752513 | tf_op jit(solution)/shard_map/while/body/eval_jaxpr/dot_general | solution.py:68
  137.4 2.1 %convolution_add_fusion.12 = f32[64,256]{1,0:T(8,128)} fusion(bf16[64,4096]{1,0:T(8,128)(2,1)} %bitcast.208, bf16[4096,256]{1,0:T(8,128)(2,1)S(1)} %get-tuple-element.468, f32[64,256]{1,0:T(8,128)} %get-tuple-element.456, pred[]{:T(512)S(6)} %compare.6), kind=kOutput, calls=%fused_computation.3.clone.1 | convolution fusion | flops 134250496 | bytes 2752513 | tf_op jit(solution)/shard_map/while/body/eval_jaxpr/dot_general | solution.py:68
  142.1 2.1 %convolution_add_fusion.12 = f32[64,256]{1,0:T(8,128)} fusion(bf16[64,4096]{1,0:T(8,128)(2,1)} %bitcast.208, bf16[4096,256]{1,0:T(8,128)(2,1)S(1)} %get-tuple-element.468, f32[64,256]{1,0:T(8,128)} %get-tuple-element.456, pred[]{:T(512)S(6)} %compare.6), kind=kOutput, calls=%fused_computation.3.clone.1 | convolution fusion | flops 134250496 | bytes 2752513 | tf_op jit(solution)/shard_map/while/body/eval_jaxpr/dot_general | solution.py:68
  146.9 2.1 %convolution_add_fusion.12 = f32[64,256]{1,0:T(8,128)} fusion(bf16[64,4096]{1,0:T(8,128)(2,1)} %bitcast.208, bf16[4096,256]{1,0:T(8,128)(2,1)S(1)} %get-tuple-element.468, f32[64,256]{1,0:T(8,128)} %get-tuple-element.456, pred[]{:T(512)S(6)} %compare.6), kind=kOutput, calls=%fused_computation.3.clone.1 | convolution fusion | flops 134250496 | bytes 2752513 | tf_op jit(solution)/shard_map/while/body/eval_jaxpr/dot_general | solution.py:68
  151.6 2.1 %convolution_add_fusion.12 = f32[64,256]{1,0:T(8,128)} fusion(bf16[64,4096]{1,0:T(8,128)(2,1)} %bitcast.208, bf16[4096,256]{1,0:T(8,128)(2,1)S(1)} %get-tuple-element.468, f32[64,256]{1,0:T(8,128)} %get-tuple-element.456, pred[]{:T(512)S(6)} %compare.6), kind=kOutput, calls=%fused_computation.3.clone.1 | convolution fusion | flops 134250496 | bytes 2752513 | tf_op jit(solution)/shard_map/while/body/eval_jaxpr/dot_general | solution.py:68
  156.3 2.1 %convolution_add_fusion.12 = f32[64,256]{1,0:T(8,128)} fusion(bf16[64,4096]{1,0:T(8,128)(2,1)} %bitcast.208, bf16[4096,256]{1,0:T(8,128)(2,1)S(1)} %get-tuple-element.468, f32[64,256]{1,0:T(8,128)} %get-tuple-element.456, pred[]{:T(512)S(6)} %compare.6), kind=kOutput, calls=%fused_computation.3.clone.1 | convolution fusion | flops 134250496 | bytes 2752513 | tf_op jit(solution)/shard_map/while/body/eval_jaxpr/dot_general | solution.py:68
  161.0 2.1 %convolution_add_fusion.12 = f32[64,256]{1,0:T(8,128)} fusion(bf16[64,4096]{1,0:T(8,128)(2,1)} %bitcast.208, bf16[4096,256]{1,0:T(8,128)(2,1)S(1)} %get-tuple-element.468, f32[64,256]{1,0:T(8,128)} %get-tuple-element.456, pred[]{:T(512)S(6)} %compare.6), kind=kOutput, calls=%fused_computation.3.clone.1 | convolution fusion | flops 134250496 | bytes 2752513 | tf_op jit(solution)/shard_map/while/body/eval_jaxpr/dot_general | solution.py:68
  165.8 2.1 %convolution_add_fusion.12 = f32[64,256]{1,0:T(8,128)} fusion(bf16[64,4096]{1,0:T(8,128)(2,1)} %bitcast.208, bf16[4096,256]{1,0:T(8,128)(2,1)S(1)} %get-tuple-element.468, f32[64,256]{1,0:T(8,128)} %get-tuple-element.456, pred[]{:T(512)S(6)} %compare.6), kind=kOutput, calls=%fused_computation.3.clone.1 | convolution fusion | flops 134250496 | bytes 2752513 | tf_op jit(solution)/shard_map/while/body/eval_jaxpr/dot_general | solution.py:68
  170.5 2.1 %convolution_add_fusion.12 = f32[64,256]{1,0:T(8,128)} fusion(bf16[64,4096]{1,0:T(8,128)(2,1)} %bitcast.208, bf16[4096,256]{1,0:T(8,128)(2,1)S(1)} %get-tuple-element.468, f32[64,256]{1,0:T(8,128)} %get-tuple-element.456, pred[]{:T(512)S(6)} %compare.6), kind=kOutput, calls=%fused_computation.3.clone.1 | convolution fusion | flops 134250496 | bytes 2752513 | tf_op jit(solution)/shard_map/while/body/eval_jaxpr/dot_general | solution.py:68
  175.2 2.1 %convolution_add_fusion.12 = f32[64,256]{1,0:T(8,128)} fusion(bf16[64,4096]{1,0:T(8,128)(2,1)} %bitcast.208, bf16[4096,256]{1,0:T(8,128)(2,1)S(1)} %get-tuple-element.468, f32[64,256]{1,0:T(8,128)} %get-tuple-element.456, pred[]{:T(512)S(6)} %compare.6), kind=kOutput, calls=%fused_computation.3.clone.1 | convolution fusion | flops 134250496 | bytes 2752513 | tf_op jit(solution)/shard_map/while/body/eval_jaxpr/dot_general | solution.py:68
  179.9 2.1 %convolution_add_fusion.12 = f32[64,256]{1,0:T(8,128)} fusion(bf16[64,4096]{1,0:T(8,128)(2,1)} %bitcast.208, bf16[4096,256]{1,0:T(8,128)(2,1)S(1)} %get-tuple-element.468, f32[64,256]{1,0:T(8,128)} %get-tuple-element.456, pred[]{:T(512)S(6)} %compare.6), kind=kOutput, calls=%fused_computation.3.clone.1 | convolution fusion | flops 134250496 | bytes 2752513 | tf_op jit(solution)/shard_map/while/body/eval_jaxpr/dot_general | solution.py:68
  184.7 2.1 %convolution_add_fusion.12 = f32[64,256]{1,0:T(8,128)} fusion(bf16[64,4096]{1,0:T(8,128)(2,1)} %bitcast.208, bf16[4096,256]{1,0:T(8,128)(2,1)S(1)} %get-tuple-element.468, f32[64,256]{1,0:T(8,128)} %get-tuple-element.456, pred[]{:T(512)S(6)} %compare.6), kind=kOutput, calls=%fused_computation.3.clone.1 | convolution fusion | flops 134250496 | bytes 2752513 | tf_op jit(solution)/shard_map/while/body/eval_jaxpr/dot_general | solution.py:68
  188.4 1.4 fusion.2
  (408 shorter events, 65.2 us)
Async XLA Ops:
  0.0 14.6 %copy-start = (bf16[8,256,256]{2,1,0:T(8,128)(2,1)S(1)}, bf16[8,256,256]{2,1,0:T(8,128)(2,1)}, u32[]{:S(2)}) copy-start(bf16[8,256,256]{2,1,0:T(8,128)(2,1)} %param.28) | copy-start | bytes 3145732
  0.0 28.7 %copy-start.2 = (bf16[16,128,128]{2,1,0:T(8,128)(2,1)S(1)}, bf16[16,128,128]{2,1,0:T(8,128)(2,1)}, u32[]{:S(2)}) copy-start(bf16[16,128,128]{2,1,0:T(8,128)(2,1)} %param.29) | copy-start | bytes 1572868
  0.0 69.4 %collective-permute-start = (bf16[8,8,256]{2,1,0:T(8,128)(2,1)}, bf16[8,8,256]{2,1,0:T(8,128)(2,1)S(1)}, u32[]{:S(2)}, u32[]{:S(2)}) collective-permute-start(bf16[8,8,256]{2,1,0:T(8,128)(2,1)} %param.20), channel_id=1, source_target_pairs={{0,16},{16,32},{32,48},{48,64},{64,80},{80,96},{96,112},{112,128},... | collective-permute-start | bytes 98312 | tf_op jit(solution)/shard_map/ppermute | solution.py:14
  2.1 67.4 %collective-permute-start.1 = (bf16[8,8,256]{2,1,0:T(8,128)(2,1)}, bf16[8,8,256]{2,1,0:T(8,128)(2,1)S(1)}, u32[]{:S(2)}, u32[]{:S(2)}) collective-permute-start(bf16[8,8,256]{2,1,0:T(8,128)(2,1)} %param.20), channel_id=1, source_target_pairs={{16,0},{32,16},{48,32},{64,48},{80,64},{96,80},{112,96},{128,112},... | collective-permute-start | bytes 98312 | tf_op jit(solution)/shard_map/ppermute | solution.py:15
  16.6 25.5 %all-to-all-start = ((f32[16,8,256]{2,1,0:T(8,128)}), f32[16,8,256]{2,1,0:T(8,128)S(1)}, u32[]{:S(2)}, u32[]{:S(2)}) async-start(f32[16,8,256]{2,1,0:T(8,128)} %convolution_bitcast_fusion.1), calls=%async_computation | async-start | bytes 262144 | tf_op jit(solution)/shard_map/all_to_all | solution.py:27
  39.7 5.1 %copy-start.9 = (s32[8,8]{1,0:T(8,128)S(1)}, s32[8,8]{1,0:T(8,128)}, u32[]{:S(2)}) copy-start(s32[8,8]{1,0:T(8,128)} %param.23) | copy-start | bytes 772
  39.7 28.7 %copy-start.7 = (s32[8,8,16]{2,1,0:T(8,128)S(1)}, s32[8,8,16]{2,1,0:T(8,128)}, u32[]{:S(2)}) copy-start(s32[8,8,16]{2,1,0:T(8,128)} %param.22) | copy-start | bytes 12292
  39.7 28.8 %copy-start.16 = (s32[1,8,8]{2,1,0:T(8,128)S(1)}, s32[1,8,8]{2,1,0:T(8,128)}, u32[]{:S(2)}) copy-start(s32[1,8,8]{2,1,0:T(8,128)} %param.26) | copy-start | bytes 772
  39.7 28.9 %copy-start.17 = (s32[1,8,8]{2,1,0:T(8,128)S(1)}, s32[1,8,8]{2,1,0:T(8,128)}, u32[]{:S(2)}) copy-start(s32[1,8,8]{2,1,0:T(8,128)} %param.25) | copy-start | bytes 772
  39.8 29.0 %copy-start.13 = (f32[128,16]{0,1:T(8,128)S(1)}, f32[128,16]{0,1:T(8,128)}, u32[]{:S(2)}) copy-start(f32[128,16]{0,1:T(8,128)} %param.34) | copy-start | bytes 24580
  39.8 29.7 %copy-start.6 = (bf16[8,8,256]{2,1,0:T(8,128)(2,1)S(1)}, bf16[8,8,256]{2,1,0:T(8,128)(2,1)}, u32[]{:S(2)}) copy-start(bf16[8,8,256]{2,1,0:T(8,128)(2,1)} %param.20) | copy-start | bytes 98308
  42.0 43.9 %copy-start.1 = (bf16[16,256,256]{2,1,0:T(8,128)(2,1)S(1)}, bf16[16,256,256]{2,1,0:T(8,128)(2,1)}, u32[]{:S(2)}) copy-start(bf16[16,256,256]{2,1,0:T(8,128)(2,1)} %param.27) | copy-start | bytes 6291460
  42.1 10.4 %collective-permute-start.4 = (bf16[8,256]{1,0:T(8,128)(2,1)S(1)}, bf16[8,256]{1,0:T(8,128)(2,1)S(1)}, u32[]{:S(2)}, u32[]{:S(2)}) collective-permute-start(bf16[8,256]{1,0:T(8,128)(2,1)S(1)} %reduce_sum.89), channel_id=1, source_target_pairs={{480,0},{496,16},{0,32},{16,48},{32,64},{48,80},{64,96},{80,112},{... | collective-permute-start | bytes 12296 | tf_op jit(solution)/shard_map/ppermute | solution.py:34
  44.8 11.6 %collective-permute-start.5 = (bf16[8,256]{1,0:T(8,128)(2,1)S(1)}, bf16[8,256]{1,0:T(8,128)(2,1)S(1)}, u32[]{:S(2)}, u32[]{:S(2)}) collective-permute-start(bf16[8,256]{1,0:T(8,128)(2,1)S(1)} %reduce_sum.89), channel_id=1, source_target_pairs={{496,0},{0,16},{16,32},{32,48},{48,64},{64,80},{80,96},{96,112},{1... | collective-permute-start | bytes 12296 | tf_op jit(solution)/shard_map/ppermute | solution.py:34
  46.8 9.7 %collective-permute-start.6 = (bf16[8,256]{1,0:T(8,128)(2,1)S(1)}, bf16[8,256]{1,0:T(8,128)(2,1)S(1)}, u32[]{:S(2)}, u32[]{:S(2)}) collective-permute-start(bf16[8,256]{1,0:T(8,128)(2,1)S(1)} %reduce_sum.89), channel_id=1, source_target_pairs={{16,0},{32,16},{48,32},{64,48},{80,64},{96,80},{112,96},{128,112},... | collective-permute-start | bytes 12296 | tf_op jit(solution)/shard_map/ppermute | solution.py:34
  52.5 5.5 %collective-permute-start.7 = (bf16[8,256]{1,0:T(8,128)(2,1)S(1)}, bf16[8,256]{1,0:T(8,128)(2,1)S(1)}, u32[]{:S(2)}, u32[]{:S(2)}) collective-permute-start(bf16[8,256]{1,0:T(8,128)(2,1)S(1)} %reduce_sum.89), channel_id=1, source_target_pairs={{32,0},{48,16},{64,32},{80,48},{96,64},{112,80},{128,96},{144,112}... | collective-permute-start | bytes 12296 | tf_op jit(solution)/shard_map/ppermute | solution.py:34
  58.8 25.4 %all-to-all-start.1 = ((bf16[16,5,8,256]{3,2,1,0:T(8,128)(2,1)}), bf16[16,5,8,256]{3,2,1,0:T(8,128)(2,1)}, u32[]{:S(2)}, u32[]{:S(2)}) async-start(bf16[16,5,8,256]{3,2,1,0:T(8,128)(2,1)} %broadcast_in_dim.208), calls=%async_computation.1 | async-start | bytes 655360 | tf_op jit(solution)/shard_map/all_to_all | solution.py:45
  69.5 7.4 %collective-permute-start.3 = (bf16[24,8,256]{2,1,0:T(8,128)(2,1)S(1)}, bf16[24,8,256]{2,1,0:T(8,128)(2,1)S(1)}, u32[]{:S(2)}, u32[]{:S(2)}) collective-permute-start(bf16[24,8,256]{2,1,0:T(8,128)(2,1)S(1)} %constant_dynamic-update-slice_fusion), channel_id=1, source_target_pairs={{1,0},{2,1},{3,2},{4,3},{5,4},{6,5},{7,6},{8,7},{9,8},{10,9},{11,1... | collective-permute-start | bytes 294920 | tf_op jit(solution)/shard_map/ppermute | solution.py:15
  74.1 10.1 %collective-permute-start.2 = (bf16[24,8,256]{2,1,0:T(8,128)(2,1)S(1)}, bf16[24,8,256]{2,1,0:T(8,128)(2,1)S(1)}, u32[]{:S(2)}, u32[]{:S(2)}) collective-permute-start(bf16[24,8,256]{2,1,0:T(8,128)(2,1)S(1)} %constant_dynamic-update-slice_fusion), channel_id=1, source_target_pairs={{0,1},{1,2},{2,3},{3,4},{4,5},{5,6},{6,7},{7,8},{8,9},{9,10},{10,1... | collective-permute-start | bytes 294920 | tf_op jit(solution)/shard_map/ppermute | solution.py:14
  104.9 81.9 %all-to-all-start.2 = ((bf16[16,8,256]{2,1,0:T(8,128)(2,1)}), bf16[16,8,256]{2,1,0:T(8,128)(2,1)S(1)}, u32[]{:S(2)}, u32[]{:S(2)}) async-start(bf16[16,8,256]{2,1,0:T(8,128)(2,1)} %broadcast_in_dim.209), calls=%async_computation.2 | async-start | bytes 131072 | tf_op jit(solution)/shard_map/all_to_all | solution.py:45
  112.6 3.3 %copy-start.11 = (s32[64,16]{0,1:T(8,128)S(1)}, s32[64,16]{0,1:T(8,128)}, u32[]{:S(2)}) copy-start(s32[64,16]{0,1:T(8,128)} %copy-done.10) | copy-start | bytes 12292 | tf_op jit(solution)/shard_map/while
  112.6 3.3 %copy-start.15 = (s32[64,16]{0,1:T(8,128)S(1)}, s32[64,16]{0,1:T(8,128)}, u32[]{:S(2)}) copy-start(s32[64,16]{0,1:T(8,128)} %copy-done.14) | copy-start | bytes 12292 | tf_op jit(solution)/shard_map/while
  117.3 3.3 %copy-start.11 = (s32[64,16]{0,1:T(8,128)S(1)}, s32[64,16]{0,1:T(8,128)}, u32[]{:S(2)}) copy-start(s32[64,16]{0,1:T(8,128)} %copy-done.10) | copy-start | bytes 12292 | tf_op jit(solution)/shard_map/while
  122.0 3.3 %copy-start.11 = (s32[64,16]{0,1:T(8,128)S(1)}, s32[64,16]{0,1:T(8,128)}, u32[]{:S(2)}) copy-start(s32[64,16]{0,1:T(8,128)} %copy-done.10) | copy-start | bytes 12292 | tf_op jit(solution)/shard_map/while
  122.0 3.3 %copy-start.15 = (s32[64,16]{0,1:T(8,128)S(1)}, s32[64,16]{0,1:T(8,128)}, u32[]{:S(2)}) copy-start(s32[64,16]{0,1:T(8,128)} %copy-done.14) | copy-start | bytes 12292 | tf_op jit(solution)/shard_map/while
  126.8 3.3 %copy-start.11 = (s32[64,16]{0,1:T(8,128)S(1)}, s32[64,16]{0,1:T(8,128)}, u32[]{:S(2)}) copy-start(s32[64,16]{0,1:T(8,128)} %copy-done.10) | copy-start | bytes 12292 | tf_op jit(solution)/shard_map/while
  126.8 3.3 %copy-start.15 = (s32[64,16]{0,1:T(8,128)S(1)}, s32[64,16]{0,1:T(8,128)}, u32[]{:S(2)}) copy-start(s32[64,16]{0,1:T(8,128)} %copy-done.14) | copy-start | bytes 12292 | tf_op jit(solution)/shard_map/while
  131.5 3.3 %copy-start.11 = (s32[64,16]{0,1:T(8,128)S(1)}, s32[64,16]{0,1:T(8,128)}, u32[]{:S(2)}) copy-start(s32[64,16]{0,1:T(8,128)} %copy-done.10) | copy-start | bytes 12292 | tf_op jit(solution)/shard_map/while
  136.2 3.3 %copy-start.11 = (s32[64,16]{0,1:T(8,128)S(1)}, s32[64,16]{0,1:T(8,128)}, u32[]{:S(2)}) copy-start(s32[64,16]{0,1:T(8,128)} %copy-done.10) | copy-start | bytes 12292 | tf_op jit(solution)/shard_map/while
  140.9 3.3 %copy-start.11 = (s32[64,16]{0,1:T(8,128)S(1)}, s32[64,16]{0,1:T(8,128)}, u32[]{:S(2)}) copy-start(s32[64,16]{0,1:T(8,128)} %copy-done.10) | copy-start | bytes 12292 | tf_op jit(solution)/shard_map/while
  145.7 3.3 %copy-start.11 = (s32[64,16]{0,1:T(8,128)S(1)}, s32[64,16]{0,1:T(8,128)}, u32[]{:S(2)}) copy-start(s32[64,16]{0,1:T(8,128)} %copy-done.10) | copy-start | bytes 12292 | tf_op jit(solution)/shard_map/while
  145.7 3.3 %copy-start.15 = (s32[64,16]{0,1:T(8,128)S(1)}, s32[64,16]{0,1:T(8,128)}, u32[]{:S(2)}) copy-start(s32[64,16]{0,1:T(8,128)} %copy-done.14) | copy-start | bytes 12292 | tf_op jit(solution)/shard_map/while
  150.4 3.3 %copy-start.11 = (s32[64,16]{0,1:T(8,128)S(1)}, s32[64,16]{0,1:T(8,128)}, u32[]{:S(2)}) copy-start(s32[64,16]{0,1:T(8,128)} %copy-done.10) | copy-start | bytes 12292 | tf_op jit(solution)/shard_map/while
  150.4 3.3 %copy-start.15 = (s32[64,16]{0,1:T(8,128)S(1)}, s32[64,16]{0,1:T(8,128)}, u32[]{:S(2)}) copy-start(s32[64,16]{0,1:T(8,128)} %copy-done.14) | copy-start | bytes 12292 | tf_op jit(solution)/shard_map/while
  155.1 3.3 %copy-start.11 = (s32[64,16]{0,1:T(8,128)S(1)}, s32[64,16]{0,1:T(8,128)}, u32[]{:S(2)}) copy-start(s32[64,16]{0,1:T(8,128)} %copy-done.10) | copy-start | bytes 12292 | tf_op jit(solution)/shard_map/while
  155.1 3.3 %copy-start.15 = (s32[64,16]{0,1:T(8,128)S(1)}, s32[64,16]{0,1:T(8,128)}, u32[]{:S(2)}) copy-start(s32[64,16]{0,1:T(8,128)} %copy-done.14) | copy-start | bytes 12292 | tf_op jit(solution)/shard_map/while
  159.8 3.3 %copy-start.11 = (s32[64,16]{0,1:T(8,128)S(1)}, s32[64,16]{0,1:T(8,128)}, u32[]{:S(2)}) copy-start(s32[64,16]{0,1:T(8,128)} %copy-done.10) | copy-start | bytes 12292 | tf_op jit(solution)/shard_map/while
  159.8 3.3 %copy-start.15 = (s32[64,16]{0,1:T(8,128)S(1)}, s32[64,16]{0,1:T(8,128)}, u32[]{:S(2)}) copy-start(s32[64,16]{0,1:T(8,128)} %copy-done.14) | copy-start | bytes 12292 | tf_op jit(solution)/shard_map/while
  164.6 3.3 %copy-start.11 = (s32[64,16]{0,1:T(8,128)S(1)}, s32[64,16]{0,1:T(8,128)}, u32[]{:S(2)}) copy-start(s32[64,16]{0,1:T(8,128)} %copy-done.10) | copy-start | bytes 12292 | tf_op jit(solution)/shard_map/while
  164.6 3.3 %copy-start.15 = (s32[64,16]{0,1:T(8,128)S(1)}, s32[64,16]{0,1:T(8,128)}, u32[]{:S(2)}) copy-start(s32[64,16]{0,1:T(8,128)} %copy-done.14) | copy-start | bytes 12292 | tf_op jit(solution)/shard_map/while
  169.3 3.3 %copy-start.11 = (s32[64,16]{0,1:T(8,128)S(1)}, s32[64,16]{0,1:T(8,128)}, u32[]{:S(2)}) copy-start(s32[64,16]{0,1:T(8,128)} %copy-done.10) | copy-start | bytes 12292 | tf_op jit(solution)/shard_map/while
  169.3 3.3 %copy-start.15 = (s32[64,16]{0,1:T(8,128)S(1)}, s32[64,16]{0,1:T(8,128)}, u32[]{:S(2)}) copy-start(s32[64,16]{0,1:T(8,128)} %copy-done.14) | copy-start | bytes 12292 | tf_op jit(solution)/shard_map/while
  174.0 3.3 %copy-start.11 = (s32[64,16]{0,1:T(8,128)S(1)}, s32[64,16]{0,1:T(8,128)}, u32[]{:S(2)}) copy-start(s32[64,16]{0,1:T(8,128)} %copy-done.10) | copy-start | bytes 12292 | tf_op jit(solution)/shard_map/while
  174.0 3.3 %copy-start.15 = (s32[64,16]{0,1:T(8,128)S(1)}, s32[64,16]{0,1:T(8,128)}, u32[]{:S(2)}) copy-start(s32[64,16]{0,1:T(8,128)} %copy-done.14) | copy-start | bytes 12292 | tf_op jit(solution)/shard_map/while
  178.7 3.3 %copy-start.11 = (s32[64,16]{0,1:T(8,128)S(1)}, s32[64,16]{0,1:T(8,128)}, u32[]{:S(2)}) copy-start(s32[64,16]{0,1:T(8,128)} %copy-done.10) | copy-start | bytes 12292 | tf_op jit(solution)/shard_map/while
  178.7 3.3 %copy-start.15 = (s32[64,16]{0,1:T(8,128)S(1)}, s32[64,16]{0,1:T(8,128)}, u32[]{:S(2)}) copy-start(s32[64,16]{0,1:T(8,128)} %copy-done.14) | copy-start | bytes 12292 | tf_op jit(solution)/shard_map/while
  183.4 3.3 %copy-start.11 = (s32[64,16]{0,1:T(8,128)S(1)}, s32[64,16]{0,1:T(8,128)}, u32[]{:S(2)}) copy-start(s32[64,16]{0,1:T(8,128)} %copy-done.10) | copy-start | bytes 12292 | tf_op jit(solution)/shard_map/while
  183.5 3.3 %copy-start.15 = (s32[64,16]{0,1:T(8,128)S(1)}, s32[64,16]{0,1:T(8,128)}, u32[]{:S(2)}) copy-start(s32[64,16]{0,1:T(8,128)} %copy-done.14) | copy-start | bytes 12292 | tf_op jit(solution)/shard_map/while
  (42 other events, 48.2 us)
where the time goes:
time: 195 us; the launch traced here: 194 us
  starting transfers between devices  59.2 us (30%)
  local copies, waits for them, and re-layouts  55.9 us (29%)
  matrix products  55.6 us (29%)
  other arithmetic  12.1 us (6%)
  waiting for transfers between devices  9.13 us (5%)
    dot_general x24, matrix products, add_slot(): return summed + jnp.dot(spread, stacked, preferred_element_type=jnp.float32)  37.1 us
    gather x24, local copies, waits for them, and re-layouts, add_slot(): picked = jnp.take(flat_window, slot_codes[:, slot_number], axis=0)  23.8 us
    while x152, local copies, waits for them, and re-layouts  23.5 us
    all_to_all x2, starting transfers between devices, sent_to_all(): return lax.all_to_all(copies, axis, split_axis=0, concat_axis=0, tiled=True)  15.9 us
    ppermute x2, starting transfers between devices, extended(): after = lax.ppermute(leading, axis, down)  15.6 us
    ppermute x4, starting transfers between devices, shifted_2(): return lax.ppermute(block, axis, route)  13.6 us
    all_to_all x1, starting transfers between devices, sum_at_owner(): lax.all_to_all(tiles, axis, split_axis=0, concat_axis=0, tiled=True)  10.1 us
    dot_general x8, matrix products, body(): jnp.einsum('zf,pfo->pzo', kernel_wide, collected_tiles, precision=lax.Pre...  9.91 us
  transfers between devices with their start and end apart: 11, of which 3 were waited for; matrix products, arithmetic and copies ran while one was open for 46% of the time, Pallas kernels for 0%

commit v1 on v0

v1 whole, which is shorter than its diff:
```python
import functools

import jax
import jax.numpy as jnp
from jax import lax
from jax.experimental import pallas as pl
from jax.experimental.pallas import tpu as pltpu
from jax.sharding import PartitionSpec as P

BF16 = jnp.bfloat16
F32 = jnp.float32
LEAVES = 64
ROWS = 72
COEFFS = 256
PARENTS = 128
OPS = 16
OCTANTS = 8
SLOTS = 16
PSLOTS = 8
MIB = 1024 * 1024


def dot(a, b):
    return jnp.dot(a, b, preferred_element_type=F32)


def dot_rows(a, b):
    return lax.dot_general(a, b, (((1,), (1,)), ((), ())), preferred_element_type=F32)


def one_hot(labels, positions):
    return jnp.where(labels == positions, 1.0, 0.0).astype(BF16)


def halves(x):
    high = x.astype(BF16)
    return high, (x - high.astype(F32)).astype(BF16)


def near_kernel(src_ref, kind_ref, count_ref, density_ref, kinds_ref, out_ref, products):
    kinds_count, side, _ = kinds_ref.shape
    tiles = density_ref.shape[0]
    stacked = kinds_ref[...].reshape(kinds_count * side, side)

    @pl.loop(0, tiles // 2)
    def _(pair):
        both = jnp.concatenate([density_ref[2 * pair], density_ref[2 * pair + 1]], axis=1)
        made = dot(stacked, both)
        for half in range(2):
            products[2 * pair + half] = made[:, half * side : (half + 1) * side].reshape(
                kinds_count, side, side
            )

    @pl.loop(0, tiles)
    def _(tile):
        def add(slot, total):
            return total + products[src_ref[tile, slot], kind_ref[tile, slot]]

        out_ref[tile] = lax.fori_loop(
            0, count_ref[tile], add, jnp.zeros((side, side), F32)
        )


def parent_kernel(own_ref, gathered_ref, shift_ref, window_ref, parents_ref):
    peers = gathered_ref.shape[0]
    sources = gathered_ref[:, :LEAVES, :].reshape(peers * LEAVES, COEFFS)
    labels = []
    for peer in range(peers):
        numbers = gathered_ref[peer, LEAVES : LEAVES + 8, :].astype(F32)
        labels.append(numbers[0:1, :LEAVES] + numbers[1:2, :LEAVES] * float(PARENTS))
    labels = jnp.concatenate(labels, axis=1).astype(jnp.int32)
    positions = lax.broadcasted_iota(jnp.int32, (PARENTS, peers * LEAVES), 0)
    total = jnp.zeros((PARENTS, COEFFS), F32)
    for octant in range(OCTANTS):
        chosen = one_hot(labels, positions + octant * PARENTS)
        total = total + dot(dot(chosen, sources).astype(BF16), shift_ref[octant])
    parents = total.astype(BF16)
    parents_ref[...] = parents
    window_ref[:PARENTS, :] = parents
    own = own_ref[0]
    for place in range(3):
        peer = lax.rem(own + place + peers - 1, peers)
        window_ref[PARENTS + place * LEAVES : PARENTS + (place + 1) * LEAVES, :] = gathered_ref[
            peer, :LEAVES, :
        ]


def op_rows(numbers, first, slots):
    rows = [numbers[first + slot : first + slot + 1, :] for slot in range(slots)]
    return jnp.concatenate(rows, axis=1)


def by_operator(rows, picked, slots):
    shape = (LEAVES, slots * LEAVES)
    same = (lax.broadcasted_iota(jnp.int32, shape, 1) % LEAVES) == lax.broadcasted_iota(
        jnp.int32, shape, 0
    )
    diagonal = jnp.where(same, rows, -1.0)
    chosen = jnp.concatenate([one_hot(diagonal, float(op)) for op in range(OPS)], axis=0)
    return dot(chosen, picked)


def final_kernel(
    codes_ref,
    ops_ref,
    eye_ref,
    pick_ref,
    lists_ref,
    own_ref,
    before_ref,
    after_ref,
    before2_ref,
    after2_ref,
    operators_ref,
    shift_ref,
    left_ref,
    right_high_ref,
    right_low_ref,
    near_ref,
    out_ref,
    staged,
):
    codes = codes_ref[...]
    peers = lists_ref.shape[0]

    blocks = 3 * LEAVES
    place = lax.broadcasted_iota(jnp.int32, (LEAVES, blocks), 1)
    picked = jnp.zeros((SLOTS * LEAVES, COEFFS), F32)
    for number, ref in enumerate((before_ref, own_ref, after_ref)):
        chosen = jnp.concatenate(
            [one_hot(codes[:, s : s + 1], place + number * blocks) for s in range(SLOTS)], axis=0
        )
        picked = picked + dot(chosen, ref[PARENTS:, :])
    leaf_rows = op_rows(dot_rows(eye_ref[...], ops_ref[...]), 0, SLOTS)
    leaf_sums = by_operator(leaf_rows, picked.astype(BF16), SLOTS)

    parent_of = codes[:, SLOTS : SLOTS + 1]
    octant_of = codes[:, SLOTS + 1 : SLOTS + 2]
    owner = one_hot(parent_of // 8, lax.broadcasted_iota(jnp.int32, (LEAVES, peers), 1))
    entries = dot(owner, lists_ref[...])
    lane = lax.broadcasted_iota(jnp.int32, (LEAVES, COEFFS), 1)
    entries = jnp.where((lane % LEAVES) // 8 == parent_of % 8, entries, 0.0).astype(BF16)
    by_leaf = dot_rows(entries, pick_ref[...]).astype(jnp.int32)
    by_slot = dot_rows(pick_ref[...], entries)
    column = lax.broadcasted_iota(jnp.int32, (LEAVES, PARENTS), 1)
    coarse = jnp.zeros((PSLOTS * LEAVES, COEFFS), F32)
    for number, ref in enumerate((before2_ref, before_ref, own_ref, after_ref, after2_ref)):
        chosen = jnp.concatenate(
            [one_hot(by_leaf[:, s : s + 1], column + number * PARENTS) for s in range(PSLOTS)],
            axis=0,
        )
        coarse = coarse + dot(chosen, ref[:PARENTS, :])
    coarse_rows = op_rows(by_slot, PSLOTS, PSLOTS)
    coarse_sums = by_operator(coarse_rows, coarse.astype(BF16), PSLOTS)

    leaf_high, leaf_low = halves(leaf_sums)
    coarse_high, coarse_low = halves(coarse_sums)
    total = jnp.zeros((4 * LEAVES, COEFFS), F32)
    for op in range(OPS):
        rows = slice(op * LEAVES, (op + 1) * LEAVES)
        stacked = jnp.concatenate(
            [leaf_high[rows], leaf_low[rows], coarse_high[rows], coarse_low[rows]], axis=0
        )
        total = total + dot(stacked, operators_ref[op])
    local = total[:LEAVES] + total[LEAVES : 2 * LEAVES]
    coarse_local = total[2 * LEAVES : 3 * LEAVES] + total[3 * LEAVES :]
    coarse_local = coarse_local.astype(BF16).astype(F32)
    for octant in range(OCTANTS):
        chosen = jnp.where(octant_of == octant, coarse_local, 0.0).astype(BF16)
        local = local + dot_rows(chosen, shift_ref[octant])

    high, low = halves(local)
    spread = dot(jnp.concatenate([high, low], axis=0), right_high_ref[...])
    spread = spread[:LEAVES] + spread[LEAVES:] + dot(high, right_low_ref[...])
    harmonics = 16
    side = out_ref.shape[1]
    for row in range(harmonics):
        staged[pl.ds(row, LEAVES, stride=harmonics), :] = spread[:, row * side : (row + 1) * side]
    left = left_ref[...]
    for pair in range(out_ref.shape[0] // 2):
        parts = []
        for tile in (2 * pair, 2 * pair + 1):
            tile_high, tile_low = halves(staged[tile * LEAVES : (tile + 1) * LEAVES, :])
            parts.append(jnp.concatenate([tile_high, tile_low, tile_high, tile_low], axis=0))
        far = dot(left, jnp.concatenate(parts, axis=1))
        for half, tile in enumerate((2 * pair, 2 * pair + 1)):
            out_ref[tile] = (near_ref[tile] + far[:, half * side : (half + 1) * side]).astype(BF16)


VMEM = pl.BlockSpec(memory_space=pltpu.VMEM)
SMEM = pl.BlockSpec(memory_space=pltpu.SMEM)


def near_call(near_src, near_kind, near_count, density, kinds):
    tiles, side, _ = density.shape
    return pl.pallas_call(
        near_kernel,
        name="near",
        out_shape=jax.ShapeDtypeStruct((tiles, side, side), F32),
        in_specs=[SMEM, SMEM, SMEM, VMEM, VMEM],
        out_specs=VMEM,
        scratch_shapes=[pltpu.VMEM((tiles, kinds.shape[0], side, side), F32)],
        compiler_params=pltpu.CompilerParams(vmem_limit_bytes=20 * MIB),
        cost_estimate=pl.CostEstimate(
            flops=4 * 10**9, bytes_accessed=2 * MIB, transcendentals=0
        ),
    )(near_src, near_kind, near_count, density, kinds)


def parent_call(own, gathered, shift_up):
    return pl.pallas_call(
        parent_kernel,
        name="parents",
        out_shape=(
            jax.ShapeDtypeStruct((PARENTS + 3 * LEAVES, COEFFS), BF16),
            jax.ShapeDtypeStruct((PARENTS, COEFFS), BF16),
        ),
        in_specs=[SMEM, VMEM, VMEM],
        out_specs=(VMEM, VMEM),
        compiler_params=pltpu.CompilerParams(vmem_limit_bytes=12 * MIB),
        cost_estimate=pl.CostEstimate(
            flops=2 * 10**9, bytes_accessed=2 * MIB, transcendentals=0
        ),
    )(own, gathered, shift_up)


def final_call(*operands):
    near = operands[-1]
    return pl.pallas_call(
        final_kernel,
        name="final",
        out_shape=jax.ShapeDtypeStruct(near.shape, BF16),
        in_specs=[VMEM] * len(operands),
        out_specs=VMEM,
        scratch_shapes=[pltpu.VMEM((LEAVES * 16, near.shape[1]), F32)],
        compiler_params=pltpu.CompilerParams(vmem_limit_bytes=32 * MIB),
        cost_estimate=pl.CostEstimate(
            flops=4 * 10**9, bytes_accessed=8 * MIB, transcendentals=0
        ),
    )(*operands)


def payload(leaf_moments, leaf_parent, leaf_octant, parent_list, parent_op):
    coarse = parent_list.reshape(1, LEAVES)
    rest = jnp.zeros((1, COEFFS - LEAVES), jnp.int32)
    numbers = jnp.concatenate(
        [
            jnp.concatenate([leaf_parent.reshape(1, LEAVES), rest], axis=1),
            jnp.concatenate([leaf_octant.reshape(1, LEAVES), rest], axis=1),
            jnp.concatenate(
                [
                    coarse // PARENTS,
                    coarse % PARENTS,
                    parent_op.reshape(1, LEAVES),
                    jnp.zeros((1, LEAVES), jnp.int32),
                ],
                axis=1,
            ),
            jnp.zeros((ROWS - LEAVES - 3, COEFFS), jnp.int32),
        ],
        axis=0,
    ).astype(BF16)
    return jnp.concatenate([leaf_moments.reshape(LEAVES, COEFFS), numbers], axis=0)


def leaf_codes(leaf_list, leaf_parent, leaf_octant):
    side = leaf_list.shape[0]
    span = 2 * side + 1
    first = lax.broadcasted_iota(jnp.int32, leaf_list.shape, 0) + leaf_list // span
    second = lax.broadcasted_iota(jnp.int32, leaf_list.shape, 1) + leaf_list % span
    window = (
        (first // side) * (3 * LEAVES)
        + (second // side) * LEAVES
        + (first % side) * side
        + second % side
    )
    return jnp.concatenate(
        [
            window.reshape(LEAVES, SLOTS),
            leaf_parent.reshape(LEAVES, 1),
            leaf_octant.reshape(LEAVES, 1),
        ],
        axis=1,
    )


def split(x):
    high = lax.reduce_precision(x, 8, 7)
    return high.astype(BF16), (x - high).astype(BF16)


def eval_tables(eval_rows, eval_cols):
    side, harmonics = eval_rows.shape
    rows = jnp.tile(eval_rows, (1, 4))
    shape = rows.shape
    rows = jnp.where(
        lax.broadcasted_iota(jnp.int32, shape, 0) // (side // 4)
        == lax.broadcasted_iota(jnp.int32, shape, 1) // harmonics,
        rows,
        0.0,
    )
    high, low = split(rows)
    left = jnp.concatenate([high, high, low, low], axis=1)
    shape = (harmonics * harmonics, harmonics * side)
    columns = jnp.where(
        lax.broadcasted_iota(jnp.int32, shape, 0) // harmonics
        == lax.broadcasted_iota(jnp.int32, shape, 1) // side,
        jnp.tile(eval_cols, (harmonics, harmonics)),
        0.0,
    )
    return left, *split(columns)


def pick_table():
    shape = (16, COEFFS)
    row = lax.broadcasted_iota(jnp.int32, shape, 0)
    lane = lax.broadcasted_iota(jnp.int32, shape, 1)
    part, slot = lane // LEAVES, lane % PSLOTS
    value = jnp.where(part == 0, 128.0, 1.0)
    hit = (part < 2) & (row == slot) | (part == 2) & (row == slot + PSLOTS)
    return jnp.where(hit, value, 0.0).astype(BF16)


def shifted(value, axis, distance):
    peers = lax.axis_size(axis)
    return lax.ppermute(value, axis, [(i, (i + distance) % peers) for i in range(peers)])


def body(
    leaf_moments,
    leaf_list,
    leaf_op,
    leaf_parent,
    leaf_octant,
    parent_list,
    parent_op,
    operators,
    shift_up,
    density,
    nearby_coulomb_kernel,
    near_src,
    near_kind,
    near_count,
    eval_rows,
    eval_cols,
):
    own = lax.axis_index("yz").astype(jnp.int32).reshape(1)
    sent = payload(leaf_moments, leaf_parent, leaf_octant, parent_list[0], parent_op[0])
    copies = jnp.broadcast_to(sent, (lax.axis_size("yz"), *sent.shape))
    gathered = lax.all_to_all(copies, "yz", split_axis=0, concat_axis=0, tiled=True)

    near = near_call(near_src, near_kind, near_count, density, nearby_coulomb_kernel)
    codes = leaf_codes(leaf_list, leaf_parent, leaf_octant)
    left, right_high, right_low = eval_tables(eval_rows, eval_cols)

    window, parents = parent_call(own, gathered, shift_up)
    before = shifted(window, "gx", 1)
    after = shifted(window, "gx", -1)
    before2 = shifted(parents, "gx", 2)
    after2 = shifted(parents, "gx", -2)
    return final_call(
        codes,
        leaf_op.reshape(LEAVES, SLOTS).astype(BF16),
        jnp.eye(SLOTS, dtype=BF16),
        pick_table(),
        gathered[:, LEAVES + 2, :],
        window,
        before,
        after,
        before2,
        after2,
        operators,
        shift_up,
        left,
        right_high,
        right_low,
        near,
    )


def solution(mesh):
    in_specs = (
        P("gx", "yz", None),
        P("gx", "yz", None),
        P("gx", "yz", None),
        P("gx", "yz"),
        P("gx", "yz"),
        P("gx", "yz", None),
        P("gx", "yz", None),
        P(),
        P(),
        P(("gx", "yz"), None, None),
        P(),
        P(("gx", "yz"), None),
        P(("gx", "yz"), None),
        P(("gx", "yz")),
        P(),
        P(),
    )
    out_specs = P(("gx", "yz"), None, None)
    return jax.shard_map(body, mesh=mesh, in_specs=in_specs, out_specs=out_specs, check_vma=False)
```

time: 195 us -> 62.8 us (0.32)
  the two profiles are of different devices: /device:TPU:4 before, /device:TPU:2 now
where the time goes in v1:
time: 62.8 us; the launch traced here: 62.2 us
  starting transfers between devices  28.4 us (45%)
  Pallas kernels  11.2 us (18%)
  waiting for transfers between devices  11.2 us (18%)
  local copies, waits for them, and re-layouts  6.66 us (11%)
  other arithmetic  4.37 us (7%)
    ppermute x4, starting transfers between devices, shifted(): lax.ppermute(value, axis, [(i, (i + distance) % peers) for i in range(pee...  19.6 us
    all_to_all x1, waiting for transfers between devices, body(): lax.all_to_all(copies, 'yz', split_axis=0, concat_axis=0, tiled=True)  9.35 us
    all_to_all x1, starting transfers between devices, body(): lax.all_to_all(copies, 'yz', split_axis=0, concat_axis=0, tiled=True)  8.77 us
    pallas_call x1, Pallas kernels, final_call(): pl.pallas_call(final_kernel, name='final', out_shape=jax.ShapeDtypeStruct...  5.69 us
    pallas_call x1, Pallas kernels, near_call(): pl.pallas_call(near_kernel, name='near', out_shape=jax.ShapeDtypeStruct((...  4.3 us
    another operation x4, other arithmetic  2.17 us
    unnamed x27, local copies, waits for them, and re-layouts  2.05 us
    ppermute x4, waiting for transfers between devices, shifted(): lax.ppermute(value, axis, [(i, (i + distance) % peers) for i in range(pee...  1.83 us
  transfers between devices with their start and end apart: 5, of which 3 were waited for; matrix products, arithmetic and copies ran while one was open for 6% of the time, Pallas kernels for 7%

profile of v1, /device:TPU:2, one launch (start us, length us, event | category | flops | bytes accessed | tf_op | source)
XLA Modules:
  0.0 62.2 jit_solution(3085927720954134871)
XLA Ops:
  0.0 0.0 copy-start.6
  0.0 0.0 copy-start.7
  0.0 0.0 copy-start.3
  0.0 0.0 copy-start.4
  0.0 0.8 %convert.27 = bf16[8,8]{1,0:T(8,128)(2,1)S(1)} convert(s32[8,8]{1,0:T(8,128)} %param.19) | non-fusion elementwise | flops 64 | bytes 384 | tf_op jit(solution)/shard_map/convert.14
  0.8 0.1 reshape.174
  0.9 0.7 %convert.28 = bf16[8,8]{1,0:T(8,128)(2,1)S(1)} convert(s32[8,8]{1,0:T(8,128)} %param.20) | non-fusion elementwise | flops 64 | bytes 384 | tf_op jit(solution)/shard_map/convert.11
  1.6 0.1 reshape.175
  1.7 0.7 %convert.31 = bf16[1,8,8]{2,1,0:T(8,128)(2,1)S(1)} convert(s32[1,8,8]{2,1,0:T(8,128)} %param.22) | non-fusion elementwise | flops 64 | bytes 384 | tf_op jit(solution)/shard_map/convert.8
  2.4 0.1 reshape_squeeze.8
  2.5 0.8 %reshape_squeeze.7 = s32[1,64]{1,0:T(1,128)S(1)} reshape(s32[1,8,8]{2,1,0:T(8,128)} %param.21) | data formatting | bytes 512 | tf_op jit(solution)/shard_map/reshape;squeeze | solution.py:244
  3.3 0.1 pad.11.clone
  3.4 0.1 reshape_maximum_fusion
  3.4 0.8 %concatenate.26 = bf16[72,256]{1,0:T(8,128)(2,1)S(1)} concatenate(bf16[64,256]{1,0:T(8,128)(2,1)} %bitcast.21, bf16[1,256]{1,0:T(2,128)(2,1)S(1)} %concatenate.23, bf16[1,256]{1,0:T(2,128)(2,1)S(1)} %concatenate.24, bf16[1,256]{1,0:T(2,128)(2,1)S(1)} %reshape_maximum_fusion, bf16[5,256]{1,0:T(8,128)(2,1)S(1)} %broadcast_in_dim.31), dimensions={0} | concatenate | bytes 73728 | tf_op jit(solution)/shard_map/concatenate | solution.py:263
  4.2 0.9 %broadcast_in_dim.32 = bf16[16,72,256]{2,1,0:T(8,128)(2,1)} broadcast(bf16[72,256]{1,0:T(8,128)(2,1)S(1)} %concatenate.26), dimensions={1,2} | broadcast | bytes 626688 | tf_op jit(solution)/shard_map/broadcast_in_dim | solution.py:349
  5.1 8.8 %all-to-all-start = ((bf16[16,72,256]{2,1,0:T(8,128)(2,1)}), bf16[16,72,256]{2,1,0:T(8,128)(2,1)S(1)}, u32[]{:S(2)}, u32[]{:S(2)}) async-start(bf16[16,72,256]{2,1,0:T(8,128)(2,1)} %broadcast_in_dim.32), calls=%async_computation | async-start | bytes 1179648 | tf_op jit(solution)/shard_map/all_to_all | solution.py:350
  13.9 0.8 %reshape.178 = s32[64,1]{1,0:T(8,128)S(1)} reshape(s32[8,8]{1,0:T(8,128)} %param.20) | data formatting | bytes 512 | tf_op jit(solution)/shard_map/reshape | solution.py:281
  14.6 0.8 %reshape.177 = s32[64,1]{1,0:T(8,128)S(1)} reshape(s32[8,8]{1,0:T(8,128)} %param.19) | data formatting | bytes 512 | tf_op jit(solution)/shard_map/reshape | solution.py:280
  15.5 0.9 %fusion.8 = s32[64,16]{1,0:T(8,128)S(1)} fusion(s32[8,8,16]{2,1,0:T(8,128)} %param.17), kind=kLoop, calls=%fused_computation.28 | loop fusion | flops 59392 | bytes 8192 | tf_op jit(solution)/shard_map/reshape | solution.py:279
  16.4 0.0 copy-done.10
  16.4 0.1 copy.36
  16.5 0.1 reduce-precision_convert_fusion.1
  16.7 0.1 pad_maximum_fusion.left_ref
  16.8 0.0 copy-done.5
  16.8 0.0 copy-done.6
  16.8 0.0 copy-done.7
  16.8 0.0 copy-done.3
  16.8 0.0 copy-done.4
  16.8 0.0 copy-start.11
  16.8 4.3 %near.1.near_ref = f32[16,128,128]{2,1,0:T(8,128)S(1)} custom-call(s32[16,16]{1,0:T(8,128)S(1)} %copy-done.5, s32[16,16]{1,0:T(8,128)S(1)} %copy-done.6, s32[16]{0:T(128)S(1)} %copy-done.7, bf16[16,128,128]{2,1,0:T(8,128)(2,1)S(1)} %copy-done.3, bf16[8,128,128]{2,1,0:T(8,128)(2,1)S(1)} %copy-done.4), custom_call_target="tpu_custom_call" | custom-call | flops 4000000000 | bytes 2097152 | tf_op jit(solution)/shard_map/near/pallas_call | solution.py:196
  21.2 0.0 copy-done.11
  21.2 0.0 copy-start.8
  21.2 0.2 tile.20
  21.4 0.8 %copy-done.8 = f32[16,128,128]{2,1,0:T(8,128)} copy-done((f32[16,128,128]{2,1,0:T(8,128)}, f32[16,128,128]{2,1,0:T(8,128)S(1)}, u32[]{:S(2)}) %copy-start.8) | copy-done | bytes 1048600
  22.2 0.9 %fusion = (bf16[256,2048]{1,0:T(8,128)(2,1)S(1)}, bf16[256,2048]{1,0:T(8,128)(2,1)S(1)}) fusion(f32[32,8,16,128]{3,2,1,0:T(8,128)S(1)} %bitcast.19, s32[2048]{0:T(1024)S(1)} %get-tuple-element.25, s32[2048]{0:T(1024)S(1)} %get-tuple-element.26, s32[256]{0:T(256)S(1)} %get-tuple-element.27, s32[256]{0:T(256)S(1)} %get-tuple-element.28, ...), kind=kLoop, calls=%fused_computation.2 | loop fusion | flops 4194304 | bytes 4215040 | tf_op jit(solution)/shard_map/convert_element_type | solution.py:289
  23.0 9.3 %all-to-all-done.gathered_ref = bf16[16,72,256]{2,1,0:T(8,128)(2,1)S(1)} async-done(((bf16[16,72,256]{2,1,0:T(8,128)(2,1)}), bf16[16,72,256]{2,1,0:T(8,128)(2,1)S(1)}, u32[]{:S(2)}, u32[]{:S(2)}) %all-to-all-start) | async-done | bytes 589856 | tf_op jit(solution)/shard_map/all_to_all | solution.py:350
  32.4 1.2 %copy-done.1 = bf16[8,256,256]{2,1,0:T(8,128)(2,1)S(1)} copy-done((bf16[8,256,256]{2,1,0:T(8,128)(2,1)S(1)}, bf16[8,256,256]{2,1,0:T(8,128)(2,1)}, u32[]{:S(2)}) %copy-start.1) | copy-done | bytes 1048600
  33.6 1.2 %parents.1 = (bf16[320,256]{1,0:T(8,128)(2,1)S(1)}, bf16[128,256]{1,0:T(8,128)(2,1)S(1)}) custom-call(s32[1]{0:T(128)} %bitcast.4.own_ref, bf16[16,72,256]{2,1,0:T(8,128)(2,1)S(1)} %all-to-all-done.gathered_ref, bf16[8,256,256]{2,1,0:T(8,128)(2,1)S(1)} %copy-done.1), custom_call_target="tpu_custom_call" | custom-call | flops 2000000000 | bytes 2097152 | tf_op jit(solution)/shard_map/parents/pallas_call | solution.py:211
  34.8 2.1 %collective-permute-start = (bf16[320,256]{1,0:T(8,128)(2,1)S(1)}, bf16[320,256]{1,0:T(8,128)(2,1)S(1)}, u32[]{:S(2)}, u32[]{:S(2)}) collective-permute-start(bf16[320,256]{1,0:T(8,128)(2,1)S(1)} %get-tuple-element.7.own_ref), channel_id=1, source_target_pairs={{0,16},{16,32},{32,48},{48,64},{64,80},{80,96},{96,112},{112,128},... | collective-permute-start | bytes 491528 | tf_op jit(solution)/shard_map/ppermute | solution.py:326
  36.9 9.6 %collective-permute-start.1 = (bf16[320,256]{1,0:T(8,128)(2,1)S(1)}, bf16[320,256]{1,0:T(8,128)(2,1)S(1)}, u32[]{:S(2)}, u32[]{:S(2)}) collective-permute-start(bf16[320,256]{1,0:T(8,128)(2,1)S(1)} %get-tuple-element.7.own_ref), channel_id=1, source_target_pairs={{0,496},{16,0},{32,16},{48,32},{64,48},{80,64},{96,80},{112,96},{1... | collective-permute-start | bytes 491528 | tf_op jit(solution)/shard_map/ppermute | solution.py:326
  46.5 0.1 pad_add_fusion.codes_ref
  46.6 1.9 %collective-permute-start.2 = (bf16[128,256]{1,0:T(8,128)(2,1)S(1)}, bf16[128,256]{1,0:T(8,128)(2,1)S(1)}, u32[]{:S(2)}, u32[]{:S(2)}) collective-permute-start(bf16[128,256]{1,0:T(8,128)(2,1)S(1)} %get-tuple-element.8), channel_id=1, source_target_pairs={{0,32},{16,48},{32,64},{48,80},{64,96},{80,112},{96,128},{112,144}... | collective-permute-start | bytes 196616 | tf_op jit(solution)/shard_map/ppermute | solution.py:326
  48.6 6.0 %collective-permute-start.3 = (bf16[128,256]{1,0:T(8,128)(2,1)S(1)}, bf16[128,256]{1,0:T(8,128)(2,1)S(1)}, u32[]{:S(2)}, u32[]{:S(2)}) collective-permute-start(bf16[128,256]{1,0:T(8,128)(2,1)S(1)} %get-tuple-element.8), channel_id=1, source_target_pairs={{0,480},{16,496},{32,0},{48,16},{64,32},{80,48},{96,64},{112,80},{... | collective-permute-start | bytes 196616 | tf_op jit(solution)/shard_map/ppermute | solution.py:326
  54.6 0.2 collective-permute-done.2.before2_ref
  54.9 1.6 %collective-permute-done.3.after2_ref = bf16[128,256]{1,0:T(8,128)(2,1)S(1)} collective-permute-done((bf16[128,256]{1,0:T(8,128)(2,1)S(1)}, bf16[128,256]{1,0:T(8,128)(2,1)S(1)}, u32[]{:S(2)}, u32[]{:S(2)}) %collective-permute-start.3) | collective-permute-done | bytes 65568 | tf_op jit(solution)/shard_map/ppermute | solution.py:326
  56.5 0.0 collective-permute-done.before_ref
  56.5 0.0 collective-permute-done.1.after_ref
  56.5 5.7 %final.1 = bf16[16,128,128]{2,1,0:T(8,128)(2,1)} custom-call(s32[64,18]{1,0:T(8,128)S(1)} %pad_add_fusion.codes_ref, bf16[64,16]{1,0:T(8,128)(2,1)S(1)} %convert_bitcast_fusion.ops_ref, bf16[16,16]{1,0:T(8,128)(2,1)S(1)} %fusion.26.eye_ref, bf16[16,256]{1,0:T(8,128)(2,1)S(1)} %select_convert_fusion.pick_ref, bf16[16,256]{1,0:T(8,128)(2,1)S(1)} %bitcast.18, ...), custom_call_target="tpu_custom_call" | custom-call | flops 4000000000 | bytes 8388608 | tf_op jit(solution)/shard_map/final/pallas_call | solution.py:229
  (33 shorter events, 0.2 us)
Async XLA Ops:
  0.0 16.4 %copy-start.10 = (s32[8,8,16]{2,1,0:T(8,128)S(1)}, s32[8,8,16]{2,1,0:T(8,128)}, u32[]{:S(2)}) copy-start(s32[8,8,16]{2,1,0:T(8,128)} %param.18) | copy-start | bytes 12292
  0.0 16.4 %copy-start.12 = (f32[128,16]{0,1:T(8,128)S(1)}, f32[128,16]{0,1:T(8,128)}, u32[]{:S(2)}) copy-start(f32[128,16]{0,1:T(8,128)} %param.30) | copy-start | bytes 24580
  0.0 16.8 %copy-start.5 = (s32[16,16]{1,0:T(8,128)S(1)}, s32[16,16]{1,0:T(8,128)}, u32[]{:S(2)}) copy-start(s32[16,16]{1,0:T(8,128)} %src_ref.1) | copy-start | bytes 3076
  0.0 16.8 %copy-start.6 = (s32[16,16]{1,0:T(8,128)S(1)}, s32[16,16]{1,0:T(8,128)}, u32[]{:S(2)}) copy-start(s32[16,16]{1,0:T(8,128)} %kind_ref.1) | copy-start | bytes 3076
  0.0 16.8 %copy-start.7 = (s32[16]{0:T(128)S(1)}, s32[16]{0:T(128)}, u32[]{:S(2)}) copy-start(s32[16]{0:T(128)} %count_ref.1) | copy-start | bytes 196
  0.0 16.8 %copy-start.3 = (bf16[16,128,128]{2,1,0:T(8,128)(2,1)S(1)}, bf16[16,128,128]{2,1,0:T(8,128)(2,1)}, u32[]{:S(2)}) copy-start(bf16[16,128,128]{2,1,0:T(8,128)(2,1)} %density_ref.1) | copy-start | bytes 1572868
  0.0 16.8 %copy-start.4 = (bf16[8,128,128]{2,1,0:T(8,128)(2,1)S(1)}, bf16[8,128,128]{2,1,0:T(8,128)(2,1)}, u32[]{:S(2)}) copy-start(bf16[8,128,128]{2,1,0:T(8,128)(2,1)} %kinds_ref.1) | copy-start | bytes 786436
  5.1 27.3 %all-to-all-start = ((bf16[16,72,256]{2,1,0:T(8,128)(2,1)}), bf16[16,72,256]{2,1,0:T(8,128)(2,1)S(1)}, u32[]{:S(2)}, u32[]{:S(2)}) async-start(bf16[16,72,256]{2,1,0:T(8,128)(2,1)} %broadcast_in_dim.32), calls=%async_computation | async-start | bytes 1179648 | tf_op jit(solution)/shard_map/all_to_all | solution.py:350
  16.8 4.3 %copy-start.11 = (f32[16,128]{1,0:T(8,128)S(1)}, f32[16,128]{1,0:T(8,128)}, u32[]{:S(2)}) copy-start(f32[16,128]{1,0:T(8,128)} %param.31) | copy-start | bytes 24580
  21.2 1.0 %copy-start.8 = (f32[16,128,128]{2,1,0:T(8,128)}, f32[16,128,128]{2,1,0:T(8,128)S(1)}, u32[]{:S(2)}) copy-start(f32[16,128,128]{2,1,0:T(8,128)S(1)} %near.1.near_ref) | copy-start | bytes 3145732
  32.4 1.2 %copy-start.1 = (bf16[8,256,256]{2,1,0:T(8,128)(2,1)S(1)}, bf16[8,256,256]{2,1,0:T(8,128)(2,1)}, u32[]{:S(2)}) copy-start(bf16[8,256,256]{2,1,0:T(8,128)(2,1)} %shift_ref.3) | copy-start | bytes 3145732
  33.6 22.9 %copy-start = (bf16[16,256,256]{2,1,0:T(8,128)(2,1)S(1)}, bf16[16,256,256]{2,1,0:T(8,128)(2,1)}, u32[]{:S(2)}) copy-start(bf16[16,256,256]{2,1,0:T(8,128)(2,1)} %operators_ref.1) | copy-start | bytes 6291460
  33.6 22.9 %copy-start.2 = (bf16[8,256,256]{2,1,0:T(8,128)(2,1)S(1)}, bf16[8,256,256]{2,1,0:T(8,128)(2,1)}, u32[]{:S(2)}) copy-start(bf16[8,256,256]{2,1,0:T(8,128)(2,1)} %shift_ref.3) | copy-start | bytes 3145732
  33.6 22.9 %copy-start.9 = (f32[16,128,128]{2,1,0:T(8,128)S(1)}, f32[16,128,128]{2,1,0:T(8,128)}, u32[]{:S(2)}) copy-start(f32[16,128,128]{2,1,0:T(8,128)} %copy-done.8) | copy-start | bytes 3145732
  34.8 21.6 %collective-permute-start = (bf16[320,256]{1,0:T(8,128)(2,1)S(1)}, bf16[320,256]{1,0:T(8,128)(2,1)S(1)}, u32[]{:S(2)}, u32[]{:S(2)}) collective-permute-start(bf16[320,256]{1,0:T(8,128)(2,1)S(1)} %get-tuple-element.7.own_ref), channel_id=1, source_target_pairs={{0,16},{16,32},{32,48},{48,64},{64,80},{80,96},{96,112},{112,128},... | collective-permute-start | bytes 491528 | tf_op jit(solution)/shard_map/ppermute | solution.py:326
  36.9 19.6 %collective-permute-start.1 = (bf16[320,256]{1,0:T(8,128)(2,1)S(1)}, bf16[320,256]{1,0:T(8,128)(2,1)S(1)}, u32[]{:S(2)}, u32[]{:S(2)}) collective-permute-start(bf16[320,256]{1,0:T(8,128)(2,1)S(1)} %get-tuple-element.7.own_ref), channel_id=1, source_target_pairs={{0,496},{16,0},{32,16},{48,32},{64,48},{80,64},{96,80},{112,96},{1... | collective-permute-start | bytes 491528 | tf_op jit(solution)/shard_map/ppermute | solution.py:326
  46.6 8.3 %collective-permute-start.2 = (bf16[128,256]{1,0:T(8,128)(2,1)S(1)}, bf16[128,256]{1,0:T(8,128)(2,1)S(1)}, u32[]{:S(2)}, u32[]{:S(2)}) collective-permute-start(bf16[128,256]{1,0:T(8,128)(2,1)S(1)} %get-tuple-element.8), channel_id=1, source_target_pairs={{0,32},{16,48},{32,64},{48,80},{64,96},{80,112},{96,128},{112,144}... | collective-permute-start | bytes 196616 | tf_op jit(solution)/shard_map/ppermute | solution.py:326
  48.6 7.9 %collective-permute-start.3 = (bf16[128,256]{1,0:T(8,128)(2,1)S(1)}, bf16[128,256]{1,0:T(8,128)(2,1)S(1)}, u32[]{:S(2)}, u32[]{:S(2)}) collective-permute-start(bf16[128,256]{1,0:T(8,128)(2,1)S(1)} %get-tuple-element.8), channel_id=1, source_target_pairs={{0,480},{16,496},{32,0},{48,16},{64,32},{80,48},{96,64},{112,80},{... | collective-permute-start | bytes 196616 | tf_op jit(solution)/shard_map/ppermute | solution.py:326

commit v2 on v1

v2 whole, which is shorter than its diff:
```python
import functools

import jax
import jax.numpy as jnp
from jax import lax
from jax.experimental import pallas as pl
from jax.experimental.pallas import tpu as pltpu
from jax.sharding import PartitionSpec as P

BF16 = jnp.bfloat16
F32 = jnp.float32
LEAVES = 64
ROWS = 136
COEFFS = 256
HALF = 128
BLOCKS = 3 * LEAVES
PARENTS = 128
OPS = 16
OCTANTS = 8
SLOTS = 16
PSLOTS = 8
MIB = 1024 * 1024


def dot(a, b):
    return jnp.dot(a, b, preferred_element_type=F32)


def dot_rows(a, b):
    return lax.dot_general(a, b, (((1,), (1,)), ((), ())), preferred_element_type=F32)


def one_hot(labels, positions):
    return jnp.where(labels == positions, 1.0, 0.0).astype(BF16)


def halves(x):
    high = x.astype(BF16)
    return high, (x - high.astype(F32)).astype(BF16)


def near_field(src_ref, kind_ref, count_ref, density_ref, kinds_ref, out_ref, products):
    kinds_count, side, _ = kinds_ref.shape
    tiles = density_ref.shape[0]
    stacked = kinds_ref[...].reshape(kinds_count * side, side)

    @pl.loop(0, tiles // 2)
    def _(pair):
        both = jnp.concatenate([density_ref[2 * pair], density_ref[2 * pair + 1]], axis=1)
        made = dot(stacked, both)
        for half in range(2):
            products[2 * pair + half] = made[:, half * side : (half + 1) * side].reshape(
                kinds_count, side, side
            )

    @pl.loop(0, tiles)
    def _(tile):
        def add(slot, total):
            return total + products[src_ref[tile, slot], kind_ref[tile, slot]]

        out_ref[tile] = lax.fori_loop(
            0, count_ref[tile], add, jnp.zeros((side, side), F32)
        )


def payload_kernel(*refs):
    sources, out_ref, held, block, in_sem, out_sem = refs[:5], refs[5], refs[6:11], *refs[11:]
    fetches = [
        pltpu.make_async_copy(source, target, in_sem.at[number])
        for number, (source, target) in enumerate(zip(sources, held))
    ]
    for fetch in fetches:
        fetch.start()
    for fetch in fetches:
        fetch.wait()
    moments_ref, parent_ref, octant_ref, list_ref, op_ref = held
    coarse = list_ref[...]
    numbers = jnp.concatenate(
        [parent_ref[...], octant_ref[...], coarse >> 7, coarse & 127, op_ref[...]], axis=0
    )
    count, side = numbers.shape
    lane = lax.broadcasted_iota(jnp.int32, (side, LEAVES), 1)
    spread = dot(
        numbers.astype(F32).astype(BF16),
        one_hot(lane % side, lax.broadcasted_iota(jnp.int32, (side, LEAVES), 0)),
    )
    lane = lax.broadcasted_iota(jnp.int32, (count, LEAVES), 1)
    row = lax.broadcasted_iota(jnp.int32, (count, LEAVES), 0)
    kept = jnp.where(lane // side == row % side, spread, 0.0)
    rows = [
        jnp.sum(kept[number * side : (number + 1) * side], axis=0, keepdims=True)
        for number in range(count // side)
    ]
    blank = jnp.zeros((1, LEAVES), F32)
    lines = [
        jnp.concatenate(pair, axis=1)
        for pair in ((rows[0], blank), (rows[1], blank), (rows[2], rows[3]), (rows[4], blank))
    ]
    lines = jnp.concatenate(lines + [jnp.zeros((4, 2 * LEAVES), F32)], axis=0).astype(BF16)
    moments = moments_ref[...]
    block[...] = jnp.concatenate([moments[:, :HALF], moments[:, HALF:], lines], axis=0)
    stores = [
        pltpu.make_async_copy(block, out_ref.at[peer], out_sem.at[peer])
        for peer in range(out_ref.shape[0])
    ]
    for store in stores:
        store.start()
    for store in stores:
        store.wait()


def count_tables(parity_ref, list_ref, op_ref, counts_ref):
    leaf_list = list_ref[...]
    side = 8
    span = 2 * side + 1
    leaf = lax.broadcasted_iota(jnp.int32, leaf_list.shape, 0)
    first = leaf // side + leaf_list // span
    second = leaf % side + leaf_list % span
    codes = (
        (first // side) * BLOCKS
        + (second // side) * LEAVES
        + (first % side) * side
        + second % side
    )
    square = (SLOTS, SLOTS)
    eye = one_hot(
        lax.broadcasted_iota(jnp.int32, square, 0), lax.broadcasted_iota(jnp.int32, square, 1)
    )
    rows = op_rows(dot_rows(eye, op_ref[...].astype(F32).astype(BF16)), 0, SLOTS)
    chosen = operator_masks(rows, SLOTS)
    place = lax.broadcasted_iota(jnp.int32, (LEAVES, BLOCKS), 1)
    parity = parity_ref[0]
    for number in range(3):
        wanted = place + (number + parity * (2 - 2 * number)) * BLOCKS
        hits = jnp.concatenate(
            [one_hot(codes[:, s : s + 1], wanted) for s in range(SLOTS)], axis=0
        )
        counts_ref[number] = dot(chosen, hits).astype(BF16)


def eval_tables(rows_ref, cols_ref, left_ref, right_high_ref, right_low_ref):
    harmonics, side = rows_ref.shape
    rows = jnp.concatenate([rows_ref[...]] * 4, axis=0)
    rows = jnp.where(
        lax.broadcasted_iota(jnp.int32, rows.shape, 0) // harmonics
        == lax.broadcasted_iota(jnp.int32, rows.shape, 1) // (side // 4),
        rows,
        0.0,
    )
    high, low = halves(rows.T)
    left_ref[...] = jnp.concatenate([high, high, low, low], axis=1)
    for ref, part in zip((right_high_ref, right_low_ref), halves(cols_ref[...])):
        ref[...] = jnp.zeros_like(ref)
        for row in range(harmonics):
            ref[row * harmonics : (row + 1) * harmonics, row * side : (row + 1) * side] = part


def column_of(ref):
    side = ref.shape[0]
    leaf = lax.broadcasted_iota(jnp.int32, (LEAVES, side), 0)
    place = lax.broadcasted_iota(jnp.int32, (LEAVES, side), 1)
    spread = dot(one_hot(leaf // side, place), ref[...].astype(F32).astype(BF16))
    kept = jnp.where(leaf % side == place, spread, 0.0)
    return jnp.sum(kept, axis=1, keepdims=True).astype(jnp.int32)


def ready_kernel(
    parity_ref,
    src_ref,
    kind_ref,
    count_ref,
    density_ref,
    kinds_ref,
    list_ref,
    op_ref,
    rows_ref,
    cols_ref,
    out_ref,
    counts_ref,
    left_ref,
    right_high_ref,
    right_low_ref,
    products,
):
    near_field(src_ref, kind_ref, count_ref, density_ref, kinds_ref, out_ref, products)
    count_tables(parity_ref, list_ref, op_ref, counts_ref)
    eval_tables(rows_ref, cols_ref, left_ref, right_high_ref, right_low_ref)


def parent_kernel(own_ref, gathered_ref, shift_ref, window_ref, parents_ref):
    peers = gathered_ref.shape[0]
    flat = (peers * LEAVES, HALF)
    sources = jnp.concatenate(
        [
            gathered_ref[:, :LEAVES, :].reshape(flat),
            gathered_ref[:, LEAVES : 2 * LEAVES, :].reshape(flat),
        ],
        axis=1,
    )
    labels = []
    for peer in range(peers):
        numbers = gathered_ref[peer, 2 * LEAVES :, :].astype(F32)
        labels.append(numbers[0:1, :LEAVES] + numbers[1:2, :LEAVES] * float(PARENTS))
    labels = jnp.concatenate(labels, axis=1).astype(jnp.int32)
    positions = lax.broadcasted_iota(jnp.int32, (PARENTS, peers * LEAVES), 0)
    ordered = [
        dot(one_hot(labels, positions + octant * PARENTS), sources).astype(BF16)
        for octant in range(OCTANTS)
    ]
    total = jnp.zeros((PARENTS, COEFFS), F32)
    for octant in range(OCTANTS):
        total = total + dot(ordered[octant], shift_ref[octant])
    parents = total.astype(BF16)
    parents_ref[...] = parents
    window_ref[:PARENTS, :] = parents
    own = own_ref[0]
    for place in range(3):
        peer = lax.rem(own + place + peers - 1, peers)
        rows = slice(PARENTS + place * LEAVES, PARENTS + (place + 1) * LEAVES)
        window_ref[rows, :HALF] = gathered_ref[peer, :LEAVES, :]
        window_ref[rows, HALF:] = gathered_ref[peer, LEAVES : 2 * LEAVES, :]


def op_rows(numbers, first, slots):
    rows = [numbers[first + slot : first + slot + 1, :] for slot in range(slots)]
    return jnp.concatenate(rows, axis=1)


def operator_masks(rows, slots):
    shape = (LEAVES, slots * LEAVES)
    same = (lax.broadcasted_iota(jnp.int32, shape, 1) % LEAVES) == lax.broadcasted_iota(
        jnp.int32, shape, 0
    )
    diagonal = jnp.where(same, rows, -1.0)
    return jnp.concatenate([one_hot(diagonal, float(op)) for op in range(OPS)], axis=0)


def pick_table():
    shape = (16, COEFFS)
    row = lax.broadcasted_iota(jnp.int32, shape, 0)
    lane = lax.broadcasted_iota(jnp.int32, shape, 1)
    part, slot = lane // LEAVES, lane % PSLOTS
    value = jnp.where(part == 0, 128.0, 1.0)
    hit = (part < 2) & (row == slot) | (part == 2) & (row == slot + PSLOTS)
    return jnp.where(hit, value, 0.0).astype(BF16)


def coarse_kernel(
    parity_ref,
    parent_ref,
    gathered_ref,
    own_ref,
    counts_ref,
    leaf_ref,
    coarse_ref,
    coarse_counts_ref,
):
    leaf_ref[...] = dot(counts_ref[1], own_ref[PARENTS:, :])
    peers = gathered_ref.shape[0]
    parent_of = column_of(parent_ref)
    pick = pick_table()
    lists = []
    for peer in range(peers):
        numbers = gathered_ref[peer, 2 * LEAVES :, :].astype(F32)
        lists.append(jnp.concatenate([numbers[2:3], numbers[3:4]], axis=1))
    lists = jnp.concatenate(lists, axis=0).astype(BF16)
    owner = one_hot(parent_of // 8, lax.broadcasted_iota(jnp.int32, (LEAVES, peers), 1))
    entries = dot(owner, lists)
    lane = lax.broadcasted_iota(jnp.int32, (LEAVES, COEFFS), 1)
    entries = jnp.where((lane % LEAVES) // 8 == parent_of % 8, entries, 0.0).astype(BF16)
    by_leaf = dot_rows(entries, pick).astype(jnp.int32)
    by_slot = dot_rows(pick, entries)
    chosen = operator_masks(op_rows(by_slot, PSLOTS, PSLOTS), PSLOTS)
    column = lax.broadcasted_iota(jnp.int32, (LEAVES, PARENTS), 1)
    parity = parity_ref[0]
    for number in range(5):
        wanted = column + (number + parity * (4 - 2 * number)) * PARENTS
        hits = jnp.concatenate(
            [one_hot(by_leaf[:, s : s + 1], wanted) for s in range(PSLOTS)], axis=0
        )
        counts = dot(chosen, hits).astype(BF16)
        if number == 2:
            coarse_ref[...] = dot(counts, own_ref[:PARENTS, :])
        else:
            lanes = (number - (number > 2)) * PARENTS
            coarse_counts_ref[:, lanes : lanes + PARENTS] = counts


def final_kernel(
    octant_ref,
    counts_ref,
    leaf_ref,
    coarse_ref,
    coarse_counts_ref,
    near2_ref,
    near1_ref,
    mate_ref,
    far2_ref,
    operators_ref,
    shift_ref,
    left_ref,
    right_high_ref,
    right_low_ref,
    near_ref,
    out_ref,
    staged,
):
    leaf_sums = (
        leaf_ref[...]
        + dot(counts_ref[0], near1_ref[PARENTS:, :])
        + dot(counts_ref[2], mate_ref[PARENTS:, :])
    )
    coarse_sums = (
        coarse_ref[...]
        + dot(
            coarse_counts_ref[:, : 2 * PARENTS],
            jnp.concatenate([near2_ref[...], near1_ref[:PARENTS, :]], axis=0),
        )
        + dot(
            coarse_counts_ref[:, 2 * PARENTS :],
            jnp.concatenate([mate_ref[:PARENTS, :], far2_ref[...]], axis=0),
        )
    )

    leaf_high, leaf_low = halves(leaf_sums)
    coarse_high, coarse_low = halves(coarse_sums)
    total = jnp.zeros((4 * LEAVES, COEFFS), F32)
    for op in range(OPS):
        rows = slice(op * LEAVES, (op + 1) * LEAVES)
        stacked = jnp.concatenate(
            [leaf_high[rows], leaf_low[rows], coarse_high[rows], coarse_low[rows]], axis=0
        )
        total = total + dot(stacked, operators_ref[op])
    local = total[:LEAVES] + total[LEAVES : 2 * LEAVES]
    coarse_local = total[2 * LEAVES : 3 * LEAVES] + total[3 * LEAVES :]
    coarse_local = coarse_local.astype(BF16).astype(F32)
    octant_of = column_of(octant_ref)
    for octant in range(OCTANTS):
        chosen = jnp.where(octant_of == octant, coarse_local, 0.0).astype(BF16)
        local = local + dot_rows(chosen, shift_ref[octant])

    high, low = halves(local)
    spread = dot(jnp.concatenate([high, low], axis=0), right_high_ref[...])
    spread = spread[:LEAVES] + spread[LEAVES:] + dot(high, right_low_ref[...])
    harmonics = 16
    side = out_ref.shape[1]
    for row in range(harmonics):
        staged[pl.ds(row, LEAVES, stride=harmonics), :] = spread[:, row * side : (row + 1) * side]
    left = left_ref[...]
    for pair in range(out_ref.shape[0] // 2):
        parts = []
        for tile in (2 * pair, 2 * pair + 1):
            tile_high, tile_low = halves(staged[tile * LEAVES : (tile + 1) * LEAVES, :])
            parts.append(jnp.concatenate([tile_high, tile_low, tile_high, tile_low], axis=0))
        far = dot(left, jnp.concatenate(parts, axis=1))
        for half, tile in enumerate((2 * pair, 2 * pair + 1)):
            out_ref[tile] = (near_ref[tile] + far[:, half * side : (half + 1) * side]).astype(BF16)


VMEM = pl.BlockSpec(memory_space=pltpu.VMEM)
SMEM = pl.BlockSpec(memory_space=pltpu.SMEM)
HBM = pl.BlockSpec(memory_space=pltpu.HBM)


def ready_call(*operands):
    density, kinds = operands[4:6]
    tiles, side, _ = density.shape
    right = jax.ShapeDtypeStruct((COEFFS, 16 * side), BF16)
    return pl.pallas_call(
        ready_kernel,
        name="ready",
        out_shape=(
            jax.ShapeDtypeStruct((tiles, side, side), F32),
            jax.ShapeDtypeStruct((3, OPS * LEAVES, BLOCKS), BF16),
            jax.ShapeDtypeStruct((side, 4 * LEAVES), BF16),
            right,
            right,
        ),
        in_specs=[SMEM] * 4 + [VMEM] * 6,
        out_specs=(VMEM,) * 5,
        scratch_shapes=[pltpu.VMEM((tiles, kinds.shape[0], side, side), F32)],
        compiler_params=pltpu.CompilerParams(vmem_limit_bytes=67043328 - 4 * MIB // 2),
        cost_estimate=pl.CostEstimate(
            flops=8 * 10**9, bytes_accessed=6 * MIB, transcendentals=0
        ),
    )(*operands)


def payload_call(peers, *operands):
    return pl.pallas_call(
        payload_kernel,
        name="payload",
        out_shape=jax.ShapeDtypeStruct((peers, ROWS, HALF), BF16),
        in_specs=[HBM] * len(operands),
        out_specs=HBM,
        scratch_shapes=[pltpu.VMEM(operand.shape, operand.dtype) for operand in operands]
        + [
            pltpu.VMEM((ROWS, HALF), BF16),
            pltpu.SemaphoreType.DMA((len(operands),)),
            pltpu.SemaphoreType.DMA((peers,)),
        ],
        compiler_params=pltpu.CompilerParams(vmem_limit_bytes=67043328),
        cost_estimate=pl.CostEstimate(
            flops=10**9, bytes_accessed=MIB, transcendentals=0
        ),
    )(*operands)


def parent_call(own, gathered, shift_up):
    return pl.pallas_call(
        parent_kernel,
        name="parents",
        out_shape=(
            jax.ShapeDtypeStruct((PARENTS + BLOCKS, COEFFS), BF16),
            jax.ShapeDtypeStruct((PARENTS, COEFFS), BF16),
        ),
        in_specs=[SMEM, VMEM, VMEM],
        out_specs=(VMEM, VMEM),
        compiler_params=pltpu.CompilerParams(vmem_limit_bytes=12 * MIB),
        cost_estimate=pl.CostEstimate(
            flops=2 * 10**9, bytes_accessed=2 * MIB, transcendentals=0
        ),
    )(own, gathered, shift_up)


def coarse_call(*operands):
    rows = OPS * LEAVES
    return pl.pallas_call(
        coarse_kernel,
        name="coarse",
        out_shape=(
            jax.ShapeDtypeStruct((rows, COEFFS), F32),
            jax.ShapeDtypeStruct((rows, COEFFS), F32),
            jax.ShapeDtypeStruct((rows, 4 * PARENTS), BF16),
        ),
        in_specs=[SMEM] + [VMEM] * (len(operands) - 1),
        out_specs=(VMEM, VMEM, VMEM),
        compiler_params=pltpu.CompilerParams(vmem_limit_bytes=16 * MIB),
        cost_estimate=pl.CostEstimate(
            flops=3 * 10**9, bytes_accessed=4 * MIB, transcendentals=0
        ),
    )(*operands)


def final_call(*operands):
    near = operands[-1]
    return pl.pallas_call(
        final_kernel,
        name="final",
        out_shape=jax.ShapeDtypeStruct(near.shape, BF16),
        in_specs=[VMEM] * len(operands),
        out_specs=VMEM,
        scratch_shapes=[pltpu.VMEM((LEAVES * 16, near.shape[1]), F32)],
        compiler_params=pltpu.CompilerParams(vmem_limit_bytes=20 * MIB),
        cost_estimate=pl.CostEstimate(
            flops=4 * 10**9, bytes_accessed=8 * MIB, transcendentals=0
        ),
    )(*operands)


def routed(value, axis, to_even, to_odd):
    peers = lax.axis_size(axis)
    route = [(i, (i + (to_odd if i % 2 else to_even)) % peers) for i in range(peers)]
    return lax.ppermute(value, axis, route)


def body(
    leaf_moments,
    leaf_list,
    leaf_op,
    leaf_parent,
    leaf_octant,
    parent_list,
    parent_op,
    operators,
    shift_up,
    density,
    nearby_coulomb_kernel,
    near_src,
    near_kind,
    near_count,
    eval_rows,
    eval_cols,
):
    own = lax.axis_index("yz").astype(jnp.int32).reshape(1)
    parity = (lax.axis_index("gx") % 2).astype(jnp.int32).reshape(1)
    sent = payload_call(
        lax.axis_size("yz"),
        leaf_moments.reshape(LEAVES, COEFFS),
        leaf_parent,
        leaf_octant,
        parent_list[0],
        parent_op[0],
    )
    gathered = lax.all_to_all(sent, "yz", split_axis=0, concat_axis=0, tiled=True)

    near, counts, left, right_high, right_low = ready_call(
        parity,
        near_src,
        near_kind,
        near_count,
        density,
        nearby_coulomb_kernel,
        leaf_list.reshape(LEAVES, SLOTS),
        leaf_op.reshape(LEAVES, SLOTS),
        eval_rows.T,
        eval_cols,
    )

    window, parents = parent_call(own, gathered, shift_up)
    near1 = routed(window, "gx", -1, 1)
    mate = routed(window, "gx", 1, -1)
    near2 = routed(parents, "gx", 2, -2)
    far2 = routed(parents, "gx", -2, 2)
    leaf, coarse, coarse_counts = coarse_call(
        parity, leaf_parent, gathered, window, counts
    )
    return final_call(
        leaf_octant,
        counts,
        leaf,
        coarse,
        coarse_counts,
        near2,
        near1,
        mate,
        far2,
        operators,
        shift_up,
        left,
        right_high,
        right_low,
        near,
    )


def solution(mesh):
    in_specs = (
        P("gx", "yz", None),
        P("gx", "yz", None),
        P("gx", "yz", None),
        P("gx", "yz"),
        P("gx", "yz"),
        P("gx", "yz", None),
        P("gx", "yz", None),
        P(),
        P(),
        P(("gx", "yz"), None, None),
        P(),
        P(("gx", "yz"), None),
        P(("gx", "yz"), None),
        P(("gx", "yz")),
        P(),
        P(),
    )
    out_specs = P(("gx", "yz"), None, None)
    return jax.shard_map(body, mesh=mesh, in_specs=in_specs, out_specs=out_specs, check_vma=False)
```

time: 62.8 us -> 58.6 us (0.933)
  the two profiles are of different devices: /device:TPU:2 before, /device:TPU:1 now
where the time goes in v2:
time: 58.6 us; the launch traced here: 58.2 us
  starting transfers between devices  29.4 us (50%)
  Pallas kernels  18.3 us (31%)
  waiting for transfers between devices  10.2 us (17%)
    ppermute x4, starting transfers between devices, routed(): return lax.ppermute(value, axis, route)  19.2 us
    all_to_all x1, starting transfers between devices, body(): lax.all_to_all(sent, 'yz', split_axis=0, concat_axis=0, tiled=True)  10.2 us
    pallas_call x1, Pallas kernels, ready_call(): pl.pallas_call(ready_kernel, name='ready', out_shape=(jax.ShapeDtypeStruc...  8.48 us
    all_to_all x1, waiting for transfers between devices, body(): lax.all_to_all(sent, 'yz', split_axis=0, concat_axis=0, tiled=True)  7.56 us
    pallas_call x1, Pallas kernels, final_call(): pl.pallas_call(final_kernel, name='final', out_shape=jax.ShapeDtypeStruct...  4.44 us
    ppermute x4, waiting for transfers between devices, routed(): return lax.ppermute(value, axis, route)  2.66 us
    pallas_call x1, Pallas kernels, coarse_call(): pl.pallas_call(coarse_kernel, name='coarse', out_shape=(jax.ShapeDtypeStr...  2.44 us
    pallas_call x1, Pallas kernels, payload_call(): pl.pallas_call(payload_kernel, name='payload', out_shape=jax.ShapeDtypeSt...  1.96 us
  transfers between devices with their start and end apart: 5, of which 2 were waited for; matrix products, arithmetic and copies ran while one was open for 0% of the time, Pallas kernels for 19%

profile of v2, /device:TPU:1, one launch (start us, length us, event | category | flops | bytes accessed | tf_op | source)
XLA Modules:
  0.0 58.2 jit_solution(8152548613076760814)
XLA Ops:
  0.0 2.0 %payload.1 = bf16[16,136,128]{2,1,0:T(8,128)(2,1)} custom-call(bf16[64,256]{1,0:T(8,128)(2,1)} %bitcast.8, s32[8,8]{1,0:T(8,128)} %parent_ref.1, s32[8,8]{1,0:T(8,128)} %octant_ref.1, s32[8,8]{1,0:T(8,128)} %bitcast.12, s32[8,8]{1,0:T(8,128)} %bitcast.13), custom_call_target="tpu_custom_call" | custom-call | flops 1000000000 | bytes 1048576 | tf_op jit(solution)/shard_map/payload/pallas_call | solution.py:390
  2.0 10.2 %all-to-all-start = ((bf16[16,136,128]{2,1,0:T(8,128)(2,1)}), bf16[16,136,128]{2,1,0:T(8,128)(2,1)S(1)}, u32[]{:S(2)}, u32[]{:S(2)}) async-start(bf16[16,136,128]{2,1,0:T(8,128)(2,1)} %payload.1), calls=%async_computation | async-start | bytes 1114112 | tf_op jit(solution)/shard_map/all_to_all | solution.py:495
  12.2 0.0 copy-start.1
  12.2 8.5 %ready.1 = (f32[16,128,128]{2,1,0:T(8,128)}, bf16[3,1024,192]{2,1,0:T(8,128)(2,1)}, bf16[128,256]{1,0:T(8,128)(2,1)}, bf16[256,2048]{1,0:T(8,128)(2,1)}, bf16[256,2048]{1,0:T(8,128)(2,1)}) custom-call(s32[1]{0:T(128)} %bitcast.parity_ref, s32[16,16]{1,0:T(8,128)} %src_ref.1, s32[16,16]{1,0:T(8,128)} %kind_ref.1, s32[16]{0:T(128)} %count_ref.1, ...), custom_call_target="tpu_custom_call" | custom-call | flops 8000000000 | bytes 6291456 | tf_op jit(solution)/shard_map/ready/pallas_call | solution.py:369
  20.7 7.6 %all-to-all-done.gathered_ref = bf16[16,136,128]{2,1,0:T(8,128)(2,1)S(1)} async-done(((bf16[16,136,128]{2,1,0:T(8,128)(2,1)}), bf16[16,136,128]{2,1,0:T(8,128)(2,1)S(1)}, u32[]{:S(2)}, u32[]{:S(2)}) %all-to-all-start) | async-done | bytes 557088 | tf_op jit(solution)/shard_map/all_to_all | solution.py:495
  28.3 0.0 copy-done.1
  28.3 0.0 copy-start.2
  28.3 0.0 copy-start.4
  28.3 1.0 %parents.1 = (bf16[320,256]{1,0:T(8,128)(2,1)S(1)}, bf16[128,256]{1,0:T(8,128)(2,1)S(1)}) custom-call(s32[1]{0:T(128)} %bitcast.7.own_ref, bf16[16,136,128]{2,1,0:T(8,128)(2,1)S(1)} %all-to-all-done.gathered_ref, bf16[8,256,256]{2,1,0:T(8,128)(2,1)S(1)} %copy-done.1), custom_call_target="tpu_custom_call" | custom-call | flops 2000000000 | bytes 2097152 | tf_op jit(solution)/shard_map/parents/pallas_call | solution.py:410
  29.3 6.6 %collective-permute-start.1 = (bf16[320,256]{1,0:T(8,128)(2,1)S(1)}, bf16[320,256]{1,0:T(8,128)(2,1)S(1)}, u32[]{:S(2)}, u32[]{:S(2)}) collective-permute-start(bf16[320,256]{1,0:T(8,128)(2,1)S(1)} %get-tuple-element.16.own_ref), channel_id=1, source_target_pairs={{0,496},{16,32},{32,16},{48,64},{64,48},{80,96},{96,80},{112,128},... | collective-permute-start | bytes 491528 | tf_op jit(solution)/shard_map/ppermute | solution.py:464
  35.9 6.4 %collective-permute-start.2 = (bf16[320,256]{1,0:T(8,128)(2,1)S(1)}, bf16[320,256]{1,0:T(8,128)(2,1)S(1)}, u32[]{:S(2)}, u32[]{:S(2)}) collective-permute-start(bf16[320,256]{1,0:T(8,128)(2,1)S(1)} %get-tuple-element.16.own_ref), channel_id=1, source_target_pairs={{0,16},{16,0},{32,48},{48,32},{64,80},{80,64},{96,112},{112,96},{1... | collective-permute-start | bytes 491528 | tf_op jit(solution)/shard_map/ppermute | solution.py:464
  42.3 4.2 %collective-permute-start = (bf16[128,256]{1,0:T(8,128)(2,1)S(1)}, bf16[128,256]{1,0:T(8,128)(2,1)S(1)}, u32[]{:S(2)}, u32[]{:S(2)}) collective-permute-start(bf16[128,256]{1,0:T(8,128)(2,1)S(1)} %get-tuple-element.20), channel_id=1, source_target_pairs={{0,32},{16,496},{32,64},{48,16},{64,96},{80,48},{96,128},{112,80},... | collective-permute-start | bytes 196616 | tf_op jit(solution)/shard_map/ppermute | solution.py:464
  46.5 1.9 %collective-permute-start.3 = (bf16[128,256]{1,0:T(8,128)(2,1)S(1)}, bf16[128,256]{1,0:T(8,128)(2,1)S(1)}, u32[]{:S(2)}, u32[]{:S(2)}) collective-permute-start(bf16[128,256]{1,0:T(8,128)(2,1)S(1)} %get-tuple-element.20), channel_id=1, source_target_pairs={{0,480},{16,48},{32,0},{48,80},{64,32},{80,112},{96,64},{112,144},... | collective-permute-start | bytes 196616 | tf_op jit(solution)/shard_map/ppermute | solution.py:464
  48.5 0.0 copy-done.2
  48.5 0.0 copy-done.4
  48.5 0.0 copy-start
  48.5 0.0 copy-start.3
  48.5 0.0 copy-start.5
  48.5 0.0 copy-start.6
  48.5 0.0 copy-start.7
  48.6 0.0 copy-start.8
  48.6 2.4 %coarse.1 = (f32[1024,256]{1,0:T(8,128)S(1)}, f32[1024,256]{1,0:T(8,128)S(1)}, bf16[1024,512]{1,0:T(8,128)(2,1)S(1)}) custom-call(s32[1]{0:T(128)} %bitcast.parity_ref, s32[8,8]{1,0:T(8,128)S(1)} %copy-done.2, bf16[16,136,128]{2,1,0:T(8,128)(2,1)S(1)} %all-to-all-done.gathered_ref, bf16[320,256]{1,0:T(8,128)(2,1)S(1)} %get-tuple-element.16.own_ref, ...), custom_call_target="tpu_custom_call" | custom-call | flops 3000000000 | bytes 4194304 | tf_op jit(solution)/shard_map/coarse/pallas_call | solution.py:428
  51.0 0.0 collective-permute-done.near2_ref
  51.0 2.6 %collective-permute-done.3.far2_ref = bf16[128,256]{1,0:T(8,128)(2,1)S(1)} collective-permute-done((bf16[128,256]{1,0:T(8,128)(2,1)S(1)}, bf16[128,256]{1,0:T(8,128)(2,1)S(1)}, u32[]{:S(2)}, u32[]{:S(2)}) %collective-permute-start.3) | collective-permute-done | bytes 65568 | tf_op jit(solution)/shard_map/ppermute | solution.py:464
  53.7 0.0 collective-permute-done.1.near1_ref
  53.7 0.0 collective-permute-done.2.mate_ref
  53.7 0.0 copy-done
  53.7 0.0 copy-done.3
  53.7 0.0 copy-done.5
  53.7 0.0 copy-done.6
  53.7 0.0 copy-done.7
  53.7 0.0 copy-done.8
  53.7 4.4 %final.1 = bf16[16,128,128]{2,1,0:T(8,128)(2,1)} custom-call(s32[8,8]{1,0:T(8,128)S(1)} %copy-done.3, bf16[3,1024,192]{2,1,0:T(8,128)(2,1)S(1)} %copy-done.4, f32[1024,256]{1,0:T(8,128)S(1)} %get-tuple-element.17.leaf_ref, f32[1024,256]{1,0:T(8,128)S(1)} %get-tuple-element.18.coarse_ref, bf16[1024,512]{1,0:T(8,128)(2,1)S(1)} %get-tuple-element.19.coarse_counts_ref, ...), custom_call_target="tpu_custom_call" | custom-call | flops 4000000000 | bytes 8388608 | tf_op jit(solution)/shard_map/final/pallas_call | solution.py:447
Async XLA Ops:
  2.0 26.3 %all-to-all-start = ((bf16[16,136,128]{2,1,0:T(8,128)(2,1)}), bf16[16,136,128]{2,1,0:T(8,128)(2,1)S(1)}, u32[]{:S(2)}, u32[]{:S(2)}) async-start(bf16[16,136,128]{2,1,0:T(8,128)(2,1)} %payload.1), calls=%async_computation | async-start | bytes 1114112 | tf_op jit(solution)/shard_map/all_to_all | solution.py:495
  12.2 16.1 %copy-start.1 = (bf16[8,256,256]{2,1,0:T(8,128)(2,1)S(1)}, bf16[8,256,256]{2,1,0:T(8,128)(2,1)}, u32[]{:S(2)}) copy-start(bf16[8,256,256]{2,1,0:T(8,128)(2,1)} %shift_ref.3) | copy-start | bytes 3145732
  28.3 20.2 %copy-start.2 = (s32[8,8]{1,0:T(8,128)S(1)}, s32[8,8]{1,0:T(8,128)}, u32[]{:S(2)}) copy-start(s32[8,8]{1,0:T(8,128)} %parent_ref.1) | copy-start | bytes 772
  28.3 20.2 %copy-start.4 = (bf16[3,1024,192]{2,1,0:T(8,128)(2,1)S(1)}, bf16[3,1024,192]{2,1,0:T(8,128)(2,1)}, u32[]{:S(2)}) copy-start(bf16[3,1024,192]{2,1,0:T(8,128)(2,1)} %get-tuple-element.15.counts_ref) | copy-start | bytes 3538948
  29.3 24.4 %collective-permute-start.1 = (bf16[320,256]{1,0:T(8,128)(2,1)S(1)}, bf16[320,256]{1,0:T(8,128)(2,1)S(1)}, u32[]{:S(2)}, u32[]{:S(2)}) collective-permute-start(bf16[320,256]{1,0:T(8,128)(2,1)S(1)} %get-tuple-element.16.own_ref), channel_id=1, source_target_pairs={{0,496},{16,32},{32,16},{48,64},{64,48},{80,96},{96,80},{112,128},... | collective-permute-start | bytes 491528 | tf_op jit(solution)/shard_map/ppermute | solution.py:464
  35.9 17.8 %collective-permute-start.2 = (bf16[320,256]{1,0:T(8,128)(2,1)S(1)}, bf16[320,256]{1,0:T(8,128)(2,1)S(1)}, u32[]{:S(2)}, u32[]{:S(2)}) collective-permute-start(bf16[320,256]{1,0:T(8,128)(2,1)S(1)} %get-tuple-element.16.own_ref), channel_id=1, source_target_pairs={{0,16},{16,0},{32,48},{48,32},{64,80},{80,64},{96,112},{112,96},{1... | collective-permute-start | bytes 491528 | tf_op jit(solution)/shard_map/ppermute | solution.py:464
  42.3 8.7 %collective-permute-start = (bf16[128,256]{1,0:T(8,128)(2,1)S(1)}, bf16[128,256]{1,0:T(8,128)(2,1)S(1)}, u32[]{:S(2)}, u32[]{:S(2)}) collective-permute-start(bf16[128,256]{1,0:T(8,128)(2,1)S(1)} %get-tuple-element.20), channel_id=1, source_target_pairs={{0,32},{16,496},{32,64},{48,16},{64,96},{80,48},{96,128},{112,80},... | collective-permute-start | bytes 196616 | tf_op jit(solution)/shard_map/ppermute | solution.py:464
  46.5 7.1 %collective-permute-start.3 = (bf16[128,256]{1,0:T(8,128)(2,1)S(1)}, bf16[128,256]{1,0:T(8,128)(2,1)S(1)}, u32[]{:S(2)}, u32[]{:S(2)}) collective-permute-start(bf16[128,256]{1,0:T(8,128)(2,1)S(1)} %get-tuple-element.20), channel_id=1, source_target_pairs={{0,480},{16,48},{32,0},{48,80},{64,32},{80,112},{96,64},{112,144},... | collective-permute-start | bytes 196616 | tf_op jit(solution)/shard_map/ppermute | solution.py:464
  48.5 5.2 %copy-start = (bf16[16,256,256]{2,1,0:T(8,128)(2,1)S(1)}, bf16[16,256,256]{2,1,0:T(8,128)(2,1)}, u32[]{:S(2)}) copy-start(bf16[16,256,256]{2,1,0:T(8,128)(2,1)} %operators_ref.1) | copy-start | bytes 6291460
  48.5 5.2 %copy-start.3 = (s32[8,8]{1,0:T(8,128)S(1)}, s32[8,8]{1,0:T(8,128)}, u32[]{:S(2)}) copy-start(s32[8,8]{1,0:T(8,128)} %octant_ref.1) | copy-start | bytes 772
  48.5 5.2 %copy-start.5 = (f32[16,128,128]{2,1,0:T(8,128)S(1)}, f32[16,128,128]{2,1,0:T(8,128)}, u32[]{:S(2)}) copy-start(f32[16,128,128]{2,1,0:T(8,128)} %get-tuple-element.24.near_ref) | copy-start | bytes 3145732
  48.5 5.2 %copy-start.6 = (bf16[256,2048]{1,0:T(8,128)(2,1)S(1)}, bf16[256,2048]{1,0:T(8,128)(2,1)}, u32[]{:S(2)}) copy-start(bf16[256,2048]{1,0:T(8,128)(2,1)} %get-tuple-element.22.right_high_ref) | copy-start | bytes 3145732
  48.5 5.2 %copy-start.7 = (bf16[256,2048]{1,0:T(8,128)(2,1)S(1)}, bf16[256,2048]{1,0:T(8,128)(2,1)}, u32[]{:S(2)}) copy-start(bf16[256,2048]{1,0:T(8,128)(2,1)} %get-tuple-element.23.right_low_ref) | copy-start | bytes 3145732
  48.6 5.2 %copy-start.8 = (bf16[128,256]{1,0:T(8,128)(2,1)S(1)}, bf16[128,256]{1,0:T(8,128)(2,1)}, u32[]{:S(2)}) copy-start(bf16[128,256]{1,0:T(8,128)(2,1)} %get-tuple-element.21.left_ref) | copy-start | bytes 196612

commit v3 on v2

--- a/solution.py
+++ b/solution.py
@@ -15,11 +15,14 @@
 HALF = 128
 BLOCKS = 3 * LEAVES
 PARENTS = 128
+EDGE = 2 * PARENTS
 OPS = 16
 OCTANTS = 8
 SLOTS = 16
 PSLOTS = 8
 MIB = 1024 * 1024
+ALL_VMEM = 67043328
+TABLE_LIMIT = 16 * MIB
 
 
 def dot(a, b):
@@ -39,7 +42,7 @@
     return high, (x - high.astype(F32)).astype(BF16)
 
 
-def near_field(src_ref, kind_ref, count_ref, density_ref, kinds_ref, out_ref, products):
+def near_kernel(src_ref, kind_ref, count_ref, density_ref, kinds_ref, out_ref, products):
     kinds_count, side, _ = kinds_ref.shape
     tiles = density_ref.shape[0]
     stacked = kinds_ref[...].reshape(kinds_count * side, side)
@@ -164,30 +167,23 @@
     return jnp.sum(kept, axis=1, keepdims=True).astype(jnp.int32)
 
 
-def ready_kernel(
+def table_kernel(
     parity_ref,
-    src_ref,
-    kind_ref,
-    count_ref,
-    density_ref,
-    kinds_ref,
     list_ref,
     op_ref,
     rows_ref,
     cols_ref,
-    out_ref,
+    _,
     counts_ref,
     left_ref,
     right_high_ref,
     right_low_ref,
-    products,
 ):
-    near_field(src_ref, kind_ref, count_ref, density_ref, kinds_ref, out_ref, products)
     count_tables(parity_ref, list_ref, op_ref, counts_ref)
     eval_tables(rows_ref, cols_ref, left_ref, right_high_ref, right_low_ref)
 
 
-def parent_kernel(own_ref, gathered_ref, shift_ref, window_ref, parents_ref):
+def partial_kernel(own_ref, gathered_ref, shift_ref, sums_ref):
     peers = gathered_ref.shape[0]
     flat = (peers * LEAVES, HALF)
     sources = jnp.concatenate(
@@ -197,28 +193,51 @@
         ],
         axis=1,
     )
-    labels = []
+    labels, lists = [], []
     for peer in range(peers):
         numbers = gathered_ref[peer, 2 * LEAVES :, :].astype(F32)
         labels.append(numbers[0:1, :LEAVES] + numbers[1:2, :LEAVES] * float(PARENTS))
+        lists.append(jnp.concatenate([numbers[2:3], numbers[3:4]], axis=1))
     labels = jnp.concatenate(labels, axis=1).astype(jnp.int32)
     positions = lax.broadcasted_iota(jnp.int32, (PARENTS, peers * LEAVES), 0)
-    ordered = [
-        dot(one_hot(labels, positions + octant * PARENTS), sources).astype(BF16)
-        for octant in range(OCTANTS)
-    ]
     total = jnp.zeros((PARENTS, COEFFS), F32)
     for octant in range(OCTANTS):
-        total = total + dot(ordered[octant], shift_ref[octant])
+        chosen = one_hot(labels, positions + octant * PARENTS)
+        total = total + dot(dot(chosen, sources).astype(BF16), shift_ref[octant])
+    high, low = halves(total)
+    sums_ref[:PARENTS, :] = high
+    sums_ref[PARENTS : 2 * PARENTS, :] = low
+    edge = jnp.where(own_ref[0] % peers < peers // 2, peers - 1, 0)
+    rows = slice(EDGE, EDGE + LEAVES)
+    sums_ref[rows, :HALF] = gathered_ref[edge, :LEAVES, :]
+    sums_ref[rows, HALF:] = gathered_ref[edge, LEAVES : 2 * LEAVES, :]
+    sums_ref[EDGE + LEAVES :, :] = jnp.concatenate(lists, axis=0).astype(BF16)
+
+
+def parent_kernel(own_ref, gathered_ref, sums_ref, other_ref, window_ref, parents_ref):
+    peers = gathered_ref.shape[0]
+    total = jnp.zeros((PARENTS, COEFFS), F32)
+    for ref in (sums_ref, other_ref):
+        total = total + (
+            ref[:PARENTS, :].astype(F32) + ref[PARENTS : 2 * PARENTS, :].astype(F32)
+        )
     parents = total.astype(BF16)
     parents_ref[...] = parents
     window_ref[:PARENTS, :] = parents
-    own = own_ref[0]
+    own = lax.rem(own_ref[0], peers)
     for place in range(3):
         peer = lax.rem(own + place + peers - 1, peers)
         rows = slice(PARENTS + place * LEAVES, PARENTS + (place + 1) * LEAVES)
         window_ref[rows, :HALF] = gathered_ref[peer, :LEAVES, :]
         window_ref[rows, HALF:] = gathered_ref[peer, LEAVES : 2 * LEAVES, :]
+
+    @pl.when(own == 0)
+    def _():
+        window_ref[PARENTS : PARENTS + LEAVES, :] = other_ref[EDGE : EDGE + LEAVES, :]
+
+    @pl.when(own == peers - 1)
+    def _():
+        window_ref[PARENTS + 2 * LEAVES :, :] = other_ref[EDGE : EDGE + LEAVES, :]
 
 
 def op_rows(numbers, first, slots):
@@ -246,25 +265,28 @@
 
 
 def coarse_kernel(
+    own_ref,
     parity_ref,
     parent_ref,
-    gathered_ref,
-    own_ref,
+    sums_ref,
+    other_ref,
+    window_ref,
     counts_ref,
     leaf_ref,
     coarse_ref,
     coarse_counts_ref,
 ):
-    leaf_ref[...] = dot(counts_ref[1], own_ref[PARENTS:, :])
-    peers = gathered_ref.shape[0]
+    leaf_ref[...] = dot(counts_ref[1], window_ref[PARENTS:, :])
     parent_of = column_of(parent_ref)
     pick = pick_table()
-    lists = []
-    for peer in range(peers):
-        numbers = gathered_ref[peer, 2 * LEAVES :, :].astype(F32)
-        lists.append(jnp.concatenate([numbers[2:3], numbers[3:4]], axis=1))
-    lists = jnp.concatenate(lists, axis=0).astype(BF16)
-    owner = one_hot(parent_of // 8, lax.broadcasted_iota(jnp.int32, (LEAVES, peers), 1))
+    lists = jnp.concatenate(
+        [ref[EDGE + LEAVES :, :].astype(F32) for ref in (sums_ref, other_ref)], axis=0
+    ).astype(BF16)
+    peers = lists.shape[0]
+    half = own_ref[0] // (peers // 2) * (peers // 2)
+    owner = one_hot(
+        (parent_of // 8 + half) % peers, lax.broadcasted_iota(jnp.int32, (LEAVES, peers), 1)
+    )
     entries = dot(owner, lists)
     lane = lax.broadcasted_iota(jnp.int32, (LEAVES, COEFFS), 1)
     entries = jnp.where((lane % LEAVES) // 8 == parent_of % 8, entries, 0.0).astype(BF16)
@@ -273,28 +295,58 @@
     chosen = operator_masks(op_rows(by_slot, PSLOTS, PSLOTS), PSLOTS)
     column = lax.broadcasted_iota(jnp.int32, (LEAVES, PARENTS), 1)
     parity = parity_ref[0]
-    for number in range(5):
+    for number, lanes in ((0, 2), (1, 0), (2, None), (3, 1), (4, 3)):
         wanted = column + (number + parity * (4 - 2 * number)) * PARENTS
         hits = jnp.concatenate(
             [one_hot(by_leaf[:, s : s + 1], wanted) for s in range(PSLOTS)], axis=0
         )
         counts = dot(chosen, hits).astype(BF16)
-        if number == 2:
-            coarse_ref[...] = dot(counts, own_ref[:PARENTS, :])
+        if lanes is None:
+            coarse_ref[...] = dot(counts, window_ref[:PARENTS, :])
         else:
-            lanes = (number - (number > 2)) * PARENTS
-            coarse_counts_ref[:, lanes : lanes + PARENTS] = counts
-
-
-def final_kernel(
-    octant_ref,
+            coarse_counts_ref[:, lanes * PARENTS : (lanes + 1) * PARENTS] = counts
+
+
+def operated(sums, operators_ref):
+    high, low = halves(sums)
+    total = jnp.zeros((2 * LEAVES, COEFFS), F32)
+    for op in range(OPS):
+        rows = slice(op * LEAVES, (op + 1) * LEAVES)
+        total = total + dot(
+            jnp.concatenate([high[rows], low[rows]], axis=0), operators_ref[op]
+        )
+    return total[:LEAVES] + total[LEAVES:]
+
+
+def leaf_kernel(
     counts_ref,
     leaf_ref,
     coarse_ref,
     coarse_counts_ref,
-    near2_ref,
     near1_ref,
     mate_ref,
+    operators_ref,
+    local_ref,
+    partial_ref,
+):
+    leaf_sums = (
+        leaf_ref[...]
+        + dot(counts_ref[0], near1_ref[PARENTS:, :])
+        + dot(counts_ref[2], mate_ref[PARENTS:, :])
+    )
+    partial_ref[...] = coarse_ref[...] + dot(
+        coarse_counts_ref[:, : 2 * PARENTS],
+        jnp.concatenate([near1_ref[:PARENTS, :], mate_ref[:PARENTS, :]], axis=0),
+    )
+    local_ref[...] = operated(leaf_sums, operators_ref)
+
+
+def final_kernel(
+    octant_ref,
+    local_ref,
+    partial_ref,
+    coarse_counts_ref,
+    near2_ref,
     far2_ref,
     operators_ref,
     shift_ref,
@@ -305,36 +357,13 @@
     out_ref,
     staged,
 ):
-    leaf_sums = (
-        leaf_ref[...]
-        + dot(counts_ref[0], near1_ref[PARENTS:, :])
-        + dot(counts_ref[2], mate_ref[PARENTS:, :])
-    )
-    coarse_sums = (
-        coarse_ref[...]
-        + dot(
-            coarse_counts_ref[:, : 2 * PARENTS],
-            jnp.concatenate([near2_ref[...], near1_ref[:PARENTS, :]], axis=0),
-        )
-        + dot(
-            coarse_counts_ref[:, 2 * PARENTS :],
-            jnp.concatenate([mate_ref[:PARENTS, :], far2_ref[...]], axis=0),
-        )
-    )
-
-    leaf_high, leaf_low = halves(leaf_sums)
-    coarse_high, coarse_low = halves(coarse_sums)
-    total = jnp.zeros((4 * LEAVES, COEFFS), F32)
-    for op in range(OPS):
-        rows = slice(op * LEAVES, (op + 1) * LEAVES)
-        stacked = jnp.concatenate(
-            [leaf_high[rows], leaf_low[rows], coarse_high[rows], coarse_low[rows]], axis=0
-        )
-        total = total + dot(stacked, operators_ref[op])
-    local = total[:LEAVES] + total[LEAVES : 2 * LEAVES]
-    coarse_local = total[2 * LEAVES : 3 * LEAVES] + total[3 * LEAVES :]
-    coarse_local = coarse_local.astype(BF16).astype(F32)
+    coarse_sums = partial_ref[...] + dot(
+        coarse_counts_ref[:, 2 * PARENTS :],
+        jnp.concatenate([near2_ref[...], far2_ref[...]], axis=0),
+    )
+    coarse_local = operated(coarse_sums, operators_ref).astype(BF16).astype(F32)
     octant_of = column_of(octant_ref)
+    local = local_ref[...]
     for octant in range(OCTANTS):
         chosen = jnp.where(octant_of == octant, coarse_local, 0.0).astype(BF16)
         local = local + dot_rows(chosen, shift_ref[octant])
@@ -362,27 +391,18 @@
 HBM = pl.BlockSpec(memory_space=pltpu.HBM)
 
 
-def ready_call(*operands):
-    density, kinds = operands[4:6]
-    tiles, side, _ = density.shape
-    right = jax.ShapeDtypeStruct((COEFFS, 16 * side), BF16)
+def call(kernel, name, outs, specs, operands, limit, flops, scratch=()):
+    out_shape = tuple(jax.ShapeDtypeStruct(shape, kind) for shape, kind in outs)
+    moved = sum(operand.size * operand.dtype.itemsize for operand in operands)
     return pl.pallas_call(
-        ready_kernel,
-        name="ready",
-        out_shape=(
-            jax.ShapeDtypeStruct((tiles, side, side), F32),
-            jax.ShapeDtypeStruct((3, OPS * LEAVES, BLOCKS), BF16),
-            jax.ShapeDtypeStruct((side, 4 * LEAVES), BF16),
-            right,
-            right,
-        ),
-        in_specs=[SMEM] * 4 + [VMEM] * 6,
-        out_specs=(VMEM,) * 5,
-        scratch_shapes=[pltpu.VMEM((tiles, kinds.shape[0], side, side), F32)],
-        compiler_params=pltpu.CompilerParams(vmem_limit_bytes=67043328 - 4 * MIB // 2),
-        cost_estimate=pl.CostEstimate(
-            flops=8 * 10**9, bytes_accessed=6 * MIB, transcendentals=0
-        ),
+        kernel,
+        name=name,
+        out_shape=out_shape,
+        in_specs=specs + [VMEM] * (len(operands) - len(specs)),
+        out_specs=(VMEM,) * len(outs),
+        scratch_shapes=list(scratch),
+        compiler_params=pltpu.CompilerParams(vmem_limit_bytes=limit),
+        cost_estimate=pl.CostEstimate(flops=flops, bytes_accessed=moved, transcendentals=0),
     )(*operands)
 
 
@@ -399,61 +419,9 @@
             pltpu.SemaphoreType.DMA((len(operands),)),
             pltpu.SemaphoreType.DMA((peers,)),
         ],
-        compiler_params=pltpu.CompilerParams(vmem_limit_bytes=67043328),
+        compiler_params=pltpu.CompilerParams(vmem_limit_bytes=ALL_VMEM),
         cost_estimate=pl.CostEstimate(
             flops=10**9, bytes_accessed=MIB, transcendentals=0
-        ),
-    )(*operands)
-
-
-def parent_call(own, gathered, shift_up):
-    return pl.pallas_call(
-        parent_kernel,
-        name="parents",
-        out_shape=(
-            jax.ShapeDtypeStruct((PARENTS + BLOCKS, COEFFS), BF16),
-            jax.ShapeDtypeStruct((PARENTS, COEFFS), BF16),
-        ),
-        in_specs=[SMEM, VMEM, VMEM],
-        out_specs=(VMEM, VMEM),
-        compiler_params=pltpu.CompilerParams(vmem_limit_bytes=12 * MIB),
-        cost_estimate=pl.CostEstimate(
-            flops=2 * 10**9, bytes_accessed=2 * MIB, transcendentals=0
-        ),
-    )(own, gathered, shift_up)
-
-
-def coarse_call(*operands):
-    rows = OPS * LEAVES
-    return pl.pallas_call(
-        coarse_kernel,
-        name="coarse",
-        out_shape=(
-            jax.ShapeDtypeStruct((rows, COEFFS), F32),
-            jax.ShapeDtypeStruct((rows, COEFFS), F32),
-            jax.ShapeDtypeStruct((rows, 4 * PARENTS), BF16),
-        ),
-        in_specs=[SMEM] + [VMEM] * (len(operands) - 1),
-        out_specs=(VMEM, VMEM, VMEM),
-        compiler_params=pltpu.CompilerParams(vmem_limit_bytes=16 * MIB),
-        cost_estimate=pl.CostEstimate(
-            flops=3 * 10**9, bytes_accessed=4 * MIB, transcendentals=0
-        ),
-    )(*operands)
-
-
-def final_call(*operands):
-    near = operands[-1]
-    return pl.pallas_call(
-        final_kernel,
-        name="final",
-        out_shape=jax.ShapeDtypeStruct(near.shape, BF16),
-        in_specs=[VMEM] * len(operands),
-        out_specs=VMEM,
-        scratch_shapes=[pltpu.VMEM((LEAVES * 16, near.shape[1]), F32)],
-        compiler_params=pltpu.CompilerParams(vmem_limit_bytes=20 * MIB),
-        cost_estimate=pl.CostEstimate(
-            flops=4 * 10**9, bytes_accessed=8 * MIB, transcendentals=0
         ),
     )(*operands)
 
@@ -484,54 +452,125 @@
 ):
     own = lax.axis_index("yz").astype(jnp.int32).reshape(1)
     parity = (lax.axis_index("gx") % 2).astype(jnp.int32).reshape(1)
+    column = lax.axis_size("yz")
+    half = column // 2
     sent = payload_call(
-        lax.axis_size("yz"),
+        half,
         leaf_moments.reshape(LEAVES, COEFFS),
         leaf_parent,
         leaf_octant,
         parent_list[0],
         parent_op[0],
     )
-    gathered = lax.all_to_all(sent, "yz", split_axis=0, concat_axis=0, tiled=True)
-
-    near, counts, left, right_high, right_low = ready_call(
-        parity,
-        near_src,
-        near_kind,
-        near_count,
-        density,
-        nearby_coulomb_kernel,
-        leaf_list.reshape(LEAVES, SLOTS),
-        leaf_op.reshape(LEAVES, SLOTS),
-        eval_rows.T,
-        eval_cols,
-    )
-
-    window, parents = parent_call(own, gathered, shift_up)
+    gathered = lax.all_to_all(
+        sent,
+        "yz",
+        split_axis=0,
+        concat_axis=0,
+        tiled=True,
+        axis_index_groups=[list(range(half)), list(range(half, column))],
+    )
+
+    tiles, side, _ = density.shape
+    kinds = nearby_coulomb_kernel.shape[0]
+    (near,) = call(
+        near_kernel,
+        "near",
+        [((tiles, side, side), F32)],
+        [SMEM] * 3,
+        (near_src, near_kind, near_count, density, nearby_coulomb_kernel),
+        ALL_VMEM - 2 * MIB,
+        4 * 10**9,
+        [pltpu.VMEM((tiles, kinds, side, side), F32)],
+    )
+    (sums,) = call(
+        partial_kernel,
+        "partial",
+        [((EDGE + LEAVES + 8, COEFFS), BF16)],
+        [SMEM],
+        (own, gathered, shift_up),
+        12 * MIB,
+        10**9,
+    )
+    other = lax.ppermute(sums, "yz", [(i, (i + half) % column) for i in range(column)])
+    counts, left, right_high, right_low = call(
+        table_kernel,
+        "table",
+        [
+            ((3, OPS * LEAVES, BLOCKS), BF16),
+            ((side, 4 * LEAVES), BF16),
+            ((COEFFS, 16 * side), BF16),
+            ((COEFFS, 16 * side), BF16),
+        ],
+        [SMEM] + [VMEM] * 4 + [pl.BlockSpec(memory_space=pl.ANY)],
+        (
+            parity,
+            leaf_list.reshape(LEAVES, SLOTS),
+            leaf_op.reshape(LEAVES, SLOTS),
+            eval_rows.T,
+            eval_cols,
+            sums,
+        ),
+        TABLE_LIMIT,
+        4 * 10**9,
+    )
+
+    window, parents = call(
+        parent_kernel,
+        "parents",
+        [((PARENTS + BLOCKS, COEFFS), BF16), ((PARENTS, COEFFS), BF16)],
+        [SMEM],
+        (own, gathered, sums, other),
+        8 * MIB,
+        10**8,
+    )
     near1 = routed(window, "gx", -1, 1)
     mate = routed(window, "gx", 1, -1)
     near2 = routed(parents, "gx", 2, -2)
     far2 = routed(parents, "gx", -2, 2)
-    leaf, coarse, coarse_counts = coarse_call(
-        parity, leaf_parent, gathered, window, counts
-    )
-    return final_call(
-        leaf_octant,
-        counts,
-        leaf,
-        coarse,
-        coarse_counts,
-        near2,
-        near1,
-        mate,
-        far2,
-        operators,
-        shift_up,
-        left,
-        right_high,
-        right_low,
-        near,
-    )
+    rows = OPS * LEAVES
+    leaf, coarse, coarse_counts = call(
+        coarse_kernel,
+        "coarse",
+        [((rows, COEFFS), F32), ((rows, COEFFS), F32), ((rows, 4 * PARENTS), BF16)],
+        [SMEM] * 2,
+        (own, parity, leaf_parent, sums, other, window, counts),
+        16 * MIB,
+        3 * 10**9,
+    )
+    local, partial = call(
+        leaf_kernel,
+        "leaf",
+        [((LEAVES, COEFFS), F32), ((rows, COEFFS), F32)],
+        [],
+        (counts, leaf, coarse, coarse_counts, near1, mate, operators),
+        16 * MIB,
+        2 * 10**9,
+    )
+    (out,) = call(
+        final_kernel,
+        "final",
+        [((tiles, side, side), BF16)],
+        [],
+        (
+            leaf_octant,
+            local,
+            partial,
+            coarse_counts,
+            near2,
+            far2,
+            operators,
+            shift_up,
+            left,
+            right_high,
+            right_low,
+            near,
+        ),
+        20 * MIB,
+        3 * 10**9,
+        [pltpu.VMEM((LEAVES * 16, side), F32)],
+    )
+    return out
 
 
 def solution(mesh):

time: 58.6 us -> 58.7 us (level)
  starting transfers between devices: 29.4 us -> 34.6 us
  waiting for transfers between devices: 10.2 us -> 5.78 us
  Pallas kernels: 18.3 us -> 17.7 us
    ppermute x0 -> x1, starting transfers between devices: none -> 5.92 us  [body(): lax.ppermute(sums, 'yz', [(i, (i + half) % column) for i in range(column)])]
    all_to_all x1, waiting for transfers between devices: 7.56 us -> 3.76 us  [body(): lax.all_to_all(sent, 'yz', split_axis=0, concat_axis=0, tiled=True, axis_...]
    all_to_all x1, starting transfers between devices: 10.2 us -> 7.65 us  [body(): lax.all_to_all(sent, 'yz', split_axis=0, concat_axis=0, tiled=True, axis_...]
    ppermute x4, starting transfers between devices: 19.2 us -> 21 us  [routed(): return lax.ppermute(value, axis, route)]
    ppermute x4, waiting for transfers between devices: 2.66 us -> 1.51 us  [routed(): return lax.ppermute(value, axis, route)]
    pallas_call x4 -> x7, Pallas kernels: 16.4 us -> 15.9 us  [call(): pl.pallas_call(kernel, name=name, out_shape=out_shape, in_specs=specs + [...]
  transfers between devices with their start and end apart: 5 -> 6, of which waited for: 2 -> 3; matrix products, arithmetic and copies ran while one was open for 0% -> 0% of each run, Pallas kernels for 19% -> 20%
where the time goes in v3:
time: 58.7 us; the launch traced here: 58.3 us
  starting transfers between devices  34.6 us (59%)
  Pallas kernels  17.7 us (30%)
  waiting for transfers between devices  5.78 us (10%)
    ppermute x4, starting transfers between devices, routed(): return lax.ppermute(value, axis, route)  21 us
    pallas_call x7, Pallas kernels, call(): pl.pallas_call(kernel, name=name, out_shape=out_shape, in_specs=specs + [...  15.9 us
    all_to_all x1, starting transfers between devices, body(): lax.all_to_all(sent, 'yz', split_axis=0, concat_axis=0, tiled=True, axis_...  7.65 us
    ppermute x1, starting transfers between devices, body(): lax.ppermute(sums, 'yz', [(i, (i + half) % column) for i in range(column)])  5.92 us
    all_to_all x1, waiting for transfers between devices, body(): lax.all_to_all(sent, 'yz', split_axis=0, concat_axis=0, tiled=True, axis_...  3.76 us
    pallas_call x1, Pallas kernels, payload_call(): pl.pallas_call(payload_kernel, name='payload', out_shape=jax.ShapeDtypeSt...  1.77 us
    ppermute x4, waiting for transfers between devices, routed(): return lax.ppermute(value, axis, route)  1.51 us
  transfers between devices with their start and end apart: 6, of which 3 were waited for; matrix products, arithmetic and copies ran while one was open for 0% of the time, Pallas kernels for 20%

profile of v3, /device:TPU:1, one launch (start us, length us, event | category | flops | bytes accessed | tf_op | source)
XLA Modules:
  0.0 58.3 jit_solution(17199208646927535913)
XLA Ops:
  0.0 1.8 %payload.1 = bf16[8,136,128]{2,1,0:T(8,128)(2,1)} custom-call(bf16[64,256]{1,0:T(8,128)(2,1)} %bitcast.11, s32[8,8]{1,0:T(8,128)} %parent_ref.1, s32[8,8]{1,0:T(8,128)} %octant_ref.1, s32[8,8]{1,0:T(8,128)} %bitcast.12, s32[8,8]{1,0:T(8,128)} %bitcast.13), custom_call_target="tpu_custom_call" | custom-call | flops 1000000000 | bytes 1048576 | tf_op jit(solution)/shard_map/payload/pallas_call | solution.py:410
  1.8 7.7 %all-to-all-start = ((bf16[8,136,128]{2,1,0:T(8,128)(2,1)}), bf16[8,136,128]{2,1,0:T(8,128)(2,1)S(1)}, u32[]{:S(2)}, u32[]{:S(2)}) async-start(bf16[8,136,128]{2,1,0:T(8,128)(2,1)} %payload.1), calls=%async_computation | async-start | bytes 557056 | tf_op jit(solution)/shard_map/all_to_all | solution.py:465
  9.4 0.0 copy-start.1
  9.4 5.8 %near.1.near_ref = f32[16,128,128]{2,1,0:T(8,128)} custom-call(s32[16,16]{1,0:T(8,128)} %src_ref.1, s32[16,16]{1,0:T(8,128)} %kind_ref.1, s32[16]{0:T(128)} %count_ref.1, bf16[16,128,128]{2,1,0:T(8,128)(2,1)} %density_ref.1, bf16[8,128,128]{2,1,0:T(8,128)(2,1)} %kinds_ref.1), custom_call_target="tpu_custom_call" | custom-call | flops 4000000000 | bytes 788544 | tf_op jit(solution)/shard_map/near/pallas_call | solution.py:397
  15.3 0.0 copy-start.2
  15.3 0.0 copy-start.3
  15.3 0.0 copy-start.4
  15.3 0.0 copy-start.5
  15.3 3.8 %all-to-all-done.gathered_ref = bf16[8,136,128]{2,1,0:T(8,128)(2,1)S(1)} async-done(((bf16[8,136,128]{2,1,0:T(8,128)(2,1)}), bf16[8,136,128]{2,1,0:T(8,128)(2,1)S(1)}, u32[]{:S(2)}, u32[]{:S(2)}) %all-to-all-start) | async-done | bytes 278560 | tf_op jit(solution)/shard_map/all_to_all | solution.py:465
  19.0 0.0 copy-done.1
  19.0 0.8 %partial.1._.sums_ref = bf16[328,256]{1,0:T(8,128)(2,1)S(1)} custom-call(s32[1]{0:T(128)} %bitcast.4.own_ref, bf16[8,136,128]{2,1,0:T(8,128)(2,1)S(1)} %all-to-all-done.gathered_ref, bf16[8,256,256]{2,1,0:T(8,128)(2,1)S(1)} %copy-done.1), custom_call_target="tpu_custom_call" | custom-call | flops 1000000000 | bytes 1327108 | tf_op jit(solution)/shard_map/partial/pallas_call | solution.py:397
  19.9 5.9 %collective-permute-start = (bf16[328,256]{1,0:T(8,128)(2,1)S(1)}, bf16[328,256]{1,0:T(8,128)(2,1)S(1)}, u32[]{:S(2)}, u32[]{:S(2)}) collective-permute-start(bf16[328,256]{1,0:T(8,128)(2,1)S(1)} %partial.1._.sums_ref), channel_id=1, source_target_pairs={{0,8},{1,9},{2,10},{3,11},{4,12},{5,13},{6,14},{7,15},{8,0},{9,1},... | collective-permute-start | bytes 503816 | tf_op jit(solution)/shard_map/ppermute | solution.py:495
  25.8 0.0 copy-done.2
  25.8 0.0 copy-done.3
  25.8 0.0 copy-done.4
  25.9 0.0 copy-done.5
  25.9 0.0 copy-start.6
  25.9 2.2 %table.1 = (bf16[3,1024,192]{2,1,0:T(8,128)(2,1)S(1)}, bf16[128,256]{1,0:T(8,128)(2,1)S(1)}, bf16[256,2048]{1,0:T(8,128)(2,1)S(1)}, bf16[256,2048]{1,0:T(8,128)(2,1)S(1)}) custom-call(s32[1]{0:T(128)} %bitcast.parity_ref, s32[64,16]{1,0:T(8,128)S(1)} %bitcast.8, s32[64,16]{1,0:T(8,128)S(1)} %bitcast.9, f32[16,128]{1,0:T(8,128)S(1)} %bitcast.10, ...), custom_call_target="tpu_custom_call" | custom-call | flops 4000000000 | bytes 192516 | tf_op jit(solution)/shard_map/table/pallas_call | solution.py:397
  28.0 0.5 collective-permute-done.other_ref
  28.6 7.5 %collective-permute-start.1 = (bf16[320,256]{1,0:T(8,128)(2,1)S(1)}, bf16[320,256]{1,0:T(8,128)(2,1)S(1)}, u32[]{:S(2)}, u32[]{:S(2)}) collective-permute-start(bf16[320,256]{1,0:T(8,128)(2,1)S(1)} %get-tuple-element.17.window_ref), channel_id=1, source_target_pairs={{0,496},{16,32},{32,16},{48,64},{64,48},{80,96},{96,80},{112,128},... | collective-permute-start | bytes 491528 | tf_op jit(solution)/shard_map/ppermute | solution.py:432
  36.2 6.6 %collective-permute-start.2 = (bf16[320,256]{1,0:T(8,128)(2,1)S(1)}, bf16[320,256]{1,0:T(8,128)(2,1)S(1)}, u32[]{:S(2)}, u32[]{:S(2)}) collective-permute-start(bf16[320,256]{1,0:T(8,128)(2,1)S(1)} %get-tuple-element.17.window_ref), channel_id=1, source_target_pairs={{0,16},{16,0},{32,48},{48,32},{64,80},{80,64},{96,112},{112,96},{1... | collective-permute-start | bytes 491528 | tf_op jit(solution)/shard_map/ppermute | solution.py:432
  42.7 5.0 %collective-permute-start.3 = (bf16[128,256]{1,0:T(8,128)(2,1)S(1)}, bf16[128,256]{1,0:T(8,128)(2,1)S(1)}, u32[]{:S(2)}, u32[]{:S(2)}) collective-permute-start(bf16[128,256]{1,0:T(8,128)(2,1)S(1)} %get-tuple-element.23), channel_id=1, source_target_pairs={{0,32},{16,496},{32,64},{48,16},{64,96},{80,48},{96,128},{112,80},... | collective-permute-start | bytes 196616 | tf_op jit(solution)/shard_map/ppermute | solution.py:432
  47.7 1.9 %collective-permute-start.4 = (bf16[128,256]{1,0:T(8,128)(2,1)S(1)}, bf16[128,256]{1,0:T(8,128)(2,1)S(1)}, u32[]{:S(2)}, u32[]{:S(2)}) collective-permute-start(bf16[128,256]{1,0:T(8,128)(2,1)S(1)} %get-tuple-element.23), channel_id=1, source_target_pairs={{0,480},{16,48},{32,0},{48,80},{64,32},{80,112},{96,64},{112,144},... | collective-permute-start | bytes 196616 | tf_op jit(solution)/shard_map/ppermute | solution.py:432
  49.7 0.0 copy-done.6
  49.7 0.0 copy-start
  49.7 2.5 %coarse.1 = (f32[1024,256]{1,0:T(8,128)S(1)}, f32[1024,256]{1,0:T(8,128)S(1)}, bf16[1024,512]{1,0:T(8,128)(2,1)S(1)}) custom-call(s32[1]{0:T(128)} %bitcast.4.own_ref, s32[1]{0:T(128)} %bitcast.parity_ref, s32[8,8]{1,0:T(8,128)S(1)} %copy-done.6, bf16[328,256]{1,0:T(8,128)(2,1)S(1)} %partial.1._.sums_ref, ...), custom_call_target="tpu_custom_call" | custom-call | flops 3000000000 | bytes 1679624 | tf_op jit(solution)/shard_map/coarse/pallas_call | solution.py:397
  52.1 0.0 collective-permute-done.1.near1_ref
  52.2 0.0 collective-permute-done.2.mate_ref
  52.2 0.0 copy-done
  52.2 0.0 copy-start.7
  52.2 0.0 copy-start.8
  52.2 1.1 %leaf.1 = (f32[64,256]{1,0:T(8,128)S(1)}, f32[1024,256]{1,0:T(8,128)S(1)}) custom-call(bf16[3,1024,192]{2,1,0:T(8,128)(2,1)S(1)} %get-tuple-element.16.counts_ref, f32[1024,256]{1,0:T(8,128)S(1)} %get-tuple-element.18.leaf_ref, f32[1024,256]{1,0:T(8,128)S(1)} %get-tuple-element.19.coarse_ref, bf16[1024,512]{1,0:T(8,128)(2,1)S(1)} %get-tuple-element.20.coarse_counts_ref, ...), custom_call_target="tpu_custom_call" | custom-call | flops 2000000000 | bytes 6750208 | tf_op jit(solution)/shard_map/leaf/pallas_call | solution.py:397
  53.3 0.0 collective-permute-done.3.near2_ref
  53.3 1.5 %collective-permute-done.4.far2_ref = bf16[128,256]{1,0:T(8,128)(2,1)S(1)} collective-permute-done((bf16[128,256]{1,0:T(8,128)(2,1)S(1)}, bf16[128,256]{1,0:T(8,128)(2,1)S(1)}, u32[]{:S(2)}, u32[]{:S(2)}) %collective-permute-start.4) | collective-permute-done | bytes 65568 | tf_op jit(solution)/shard_map/ppermute | solution.py:432
  54.8 0.0 copy-done.7
  54.8 0.0 copy-done.8
  54.9 3.4 %final.1 = bf16[16,128,128]{2,1,0:T(8,128)(2,1)} custom-call(s32[8,8]{1,0:T(8,128)S(1)} %copy-done.7, f32[64,256]{1,0:T(8,128)S(1)} %get-tuple-element.21.local_ref, f32[1024,256]{1,0:T(8,128)S(1)} %get-tuple-element.22.partial_ref, bf16[1024,512]{1,0:T(8,128)(2,1)S(1)} %get-tuple-element.20.coarse_counts_ref, ...), custom_call_target="tpu_custom_call" | custom-call | flops 3000000000 | bytes 8651008 | tf_op jit(solution)/shard_map/final/pallas_call | solution.py:397
  (1 shorter events, 0.0 us)
Async XLA Ops:
  1.8 17.3 %all-to-all-start = ((bf16[8,136,128]{2,1,0:T(8,128)(2,1)}), bf16[8,136,128]{2,1,0:T(8,128)(2,1)S(1)}, u32[]{:S(2)}, u32[]{:S(2)}) async-start(bf16[8,136,128]{2,1,0:T(8,128)(2,1)} %payload.1), calls=%async_computation | async-start | bytes 557056 | tf_op jit(solution)/shard_map/all_to_all | solution.py:465
  9.4 9.6 %copy-start.1 = (bf16[8,256,256]{2,1,0:T(8,128)(2,1)S(1)}, bf16[8,256,256]{2,1,0:T(8,128)(2,1)}, u32[]{:S(2)}) copy-start(bf16[8,256,256]{2,1,0:T(8,128)(2,1)} %shift_ref.3) | copy-start | bytes 3145732
  15.3 10.6 %copy-start.2 = (s32[8,8,16]{2,1,0:T(8,128)S(1)}, s32[8,8,16]{2,1,0:T(8,128)}, u32[]{:S(2)}) copy-start(s32[8,8,16]{2,1,0:T(8,128)} %param.17) | copy-start | bytes 12292
  15.3 10.6 %copy-start.3 = (s32[8,8,16]{2,1,0:T(8,128)S(1)}, s32[8,8,16]{2,1,0:T(8,128)}, u32[]{:S(2)}) copy-start(s32[8,8,16]{2,1,0:T(8,128)} %param.18) | copy-start | bytes 12292
  15.3 10.6 %copy-start.4 = (f32[128,16]{0,1:T(8,128)S(1)}, f32[128,16]{0,1:T(8,128)}, u32[]{:S(2)}) copy-start(f32[128,16]{0,1:T(8,128)} %param.30) | copy-start | bytes 24580
  15.3 10.6 %copy-start.5 = (f32[16,128]{1,0:T(8,128)S(1)}, f32[16,128]{1,0:T(8,128)}, u32[]{:S(2)}) copy-start(f32[16,128]{1,0:T(8,128)} %cols_ref.1) | copy-start | bytes 24580
  19.9 8.7 %collective-permute-start = (bf16[328,256]{1,0:T(8,128)(2,1)S(1)}, bf16[328,256]{1,0:T(8,128)(2,1)S(1)}, u32[]{:S(2)}, u32[]{:S(2)}) collective-permute-start(bf16[328,256]{1,0:T(8,128)(2,1)S(1)} %partial.1._.sums_ref), channel_id=1, source_target_pairs={{0,8},{1,9},{2,10},{3,11},{4,12},{5,13},{6,14},{7,15},{8,0},{9,1},... | collective-permute-start | bytes 503816 | tf_op jit(solution)/shard_map/ppermute | solution.py:495
  25.9 23.8 %copy-start.6 = (s32[8,8]{1,0:T(8,128)S(1)}, s32[8,8]{1,0:T(8,128)}, u32[]{:S(2)}) copy-start(s32[8,8]{1,0:T(8,128)} %parent_ref.1) | copy-start | bytes 772
  28.6 23.5 %collective-permute-start.1 = (bf16[320,256]{1,0:T(8,128)(2,1)S(1)}, bf16[320,256]{1,0:T(8,128)(2,1)S(1)}, u32[]{:S(2)}, u32[]{:S(2)}) collective-permute-start(bf16[320,256]{1,0:T(8,128)(2,1)S(1)} %get-tuple-element.17.window_ref), channel_id=1, source_target_pairs={{0,496},{16,32},{32,16},{48,64},{64,48},{80,96},{96,80},{112,128},... | collective-permute-start | bytes 491528 | tf_op jit(solution)/shard_map/ppermute | solution.py:432
  36.2 16.0 %collective-permute-start.2 = (bf16[320,256]{1,0:T(8,128)(2,1)S(1)}, bf16[320,256]{1,0:T(8,128)(2,1)S(1)}, u32[]{:S(2)}, u32[]{:S(2)}) collective-permute-start(bf16[320,256]{1,0:T(8,128)(2,1)S(1)} %get-tuple-element.17.window_ref), channel_id=1, source_target_pairs={{0,16},{16,0},{32,48},{48,32},{64,80},{80,64},{96,112},{112,96},{1... | collective-permute-start | bytes 491528 | tf_op jit(solution)/shard_map/ppermute | solution.py:432
  42.7 10.6 %collective-permute-start.3 = (bf16[128,256]{1,0:T(8,128)(2,1)S(1)}, bf16[128,256]{1,0:T(8,128)(2,1)S(1)}, u32[]{:S(2)}, u32[]{:S(2)}) collective-permute-start(bf16[128,256]{1,0:T(8,128)(2,1)S(1)} %get-tuple-element.23), channel_id=1, source_target_pairs={{0,32},{16,496},{32,64},{48,16},{64,96},{80,48},{96,128},{112,80},... | collective-permute-start | bytes 196616 | tf_op jit(solution)/shard_map/ppermute | solution.py:432
  47.7 7.1 %collective-permute-start.4 = (bf16[128,256]{1,0:T(8,128)(2,1)S(1)}, bf16[128,256]{1,0:T(8,128)(2,1)S(1)}, u32[]{:S(2)}, u32[]{:S(2)}) collective-permute-start(bf16[128,256]{1,0:T(8,128)(2,1)S(1)} %get-tuple-element.23), channel_id=1, source_target_pairs={{0,480},{16,48},{32,0},{48,80},{64,32},{80,112},{96,64},{112,144},... | collective-permute-start | bytes 196616 | tf_op jit(solution)/shard_map/ppermute | solution.py:432
  49.7 2.5 %copy-start = (bf16[16,256,256]{2,1,0:T(8,128)(2,1)S(1)}, bf16[16,256,256]{2,1,0:T(8,128)(2,1)}, u32[]{:S(2)}) copy-start(bf16[16,256,256]{2,1,0:T(8,128)(2,1)} %operators_ref.3) | copy-start | bytes 6291460
  52.2 2.7 %copy-start.7 = (s32[8,8]{1,0:T(8,128)S(1)}, s32[8,8]{1,0:T(8,128)}, u32[]{:S(2)}) copy-start(s32[8,8]{1,0:T(8,128)} %octant_ref.1) | copy-start | bytes 772
  52.2 2.7 %copy-start.8 = (f32[16,128,128]{2,1,0:T(8,128)S(1)}, f32[16,128,128]{2,1,0:T(8,128)}, u32[]{:S(2)}) copy-start(f32[16,128,128]{2,1,0:T(8,128)} %near.1.near_ref) | copy-start | bytes 3145732

commit v4 on v2

--- a/solution.py
+++ b/solution.py
@@ -1,5 +1,3 @@
-import functools
-
 import jax
 import jax.numpy as jnp
 from jax import lax
@@ -71,9 +69,25 @@
     ]
     for fetch in fetches:
         fetch.start()
-    for fetch in fetches:
+    fetches[0].wait()
+    moments_ref, parent_ref, octant_ref, list_ref, op_ref = held
+    block[:LEAVES, :] = moments_ref[:, :HALF]
+    block[LEAVES : 2 * LEAVES, :] = moments_ref[:, HALF:]
+    peers = out_ref.shape[0]
+    stores = []
+    for part, rows in enumerate((slice(0, 2 * LEAVES), slice(2 * LEAVES, ROWS))):
+        stores.append(
+            [
+                pltpu.make_async_copy(
+                    block.at[rows], out_ref.at[peer, rows], out_sem.at[part, peer]
+                )
+                for peer in range(peers)
+            ]
+        )
+    for store in stores[0]:
+        store.start()
+    for fetch in fetches[1:]:
         fetch.wait()
-    moments_ref, parent_ref, octant_ref, list_ref, op_ref = held
     coarse = list_ref[...]
     numbers = jnp.concatenate(
         [parent_ref[...], octant_ref[...], coarse >> 7, coarse & 127, op_ref[...]], axis=0
@@ -97,15 +111,10 @@
         for pair in ((rows[0], blank), (rows[1], blank), (rows[2], rows[3]), (rows[4], blank))
     ]
     lines = jnp.concatenate(lines + [jnp.zeros((4, 2 * LEAVES), F32)], axis=0).astype(BF16)
-    moments = moments_ref[...]
-    block[...] = jnp.concatenate([moments[:, :HALF], moments[:, HALF:], lines], axis=0)
-    stores = [
-        pltpu.make_async_copy(block, out_ref.at[peer], out_sem.at[peer])
-        for peer in range(out_ref.shape[0])
-    ]
-    for store in stores:
+    block[2 * LEAVES :, :] = lines
+    for store in stores[1]:
         store.start()
-    for store in stores:
+    for store in stores[0] + stores[1]:
         store.wait()
 
 
@@ -397,7 +406,7 @@
         + [
             pltpu.VMEM((ROWS, HALF), BF16),
             pltpu.SemaphoreType.DMA((len(operands),)),
-            pltpu.SemaphoreType.DMA((peers,)),
+            pltpu.SemaphoreType.DMA((2, peers)),
         ],
         compiler_params=pltpu.CompilerParams(vmem_limit_bytes=67043328),
         cost_estimate=pl.CostEstimate(
@@ -508,10 +517,10 @@
     )
 
     window, parents = parent_call(own, gathered, shift_up)
+    near2 = routed(parents, "gx", 2, -2)
+    far2 = routed(parents, "gx", -2, 2)
     near1 = routed(window, "gx", -1, 1)
     mate = routed(window, "gx", 1, -1)
-    near2 = routed(parents, "gx", 2, -2)
-    far2 = routed(parents, "gx", -2, 2)
     leaf, coarse, coarse_counts = coarse_call(
         parity, leaf_parent, gathered, window, counts
     )

time: 58.6 us -> 58.6 us (level)
  Pallas kernels: 18.3 us -> 19.2 us
  waiting for transfers between devices: 10.2 us -> 9.31 us
    all_to_all x1, waiting for transfers between devices: 7.56 us -> 6.65 us  [body(): lax.all_to_all(sent, 'yz', split_axis=0, concat_axis=0, tiled=True)]
    pallas_call x1, Pallas kernels: 8.48 us -> 9.39 us  [ready_call(): pl.pallas_call(ready_kernel, name='ready', out_shape=(jax.ShapeDtypeStruc...]
  transfers between devices with their start and end apart: 5 -> 5, of which waited for: 2 -> 2; matrix products, arithmetic and copies ran while one was open for 0% -> 0% of each run, Pallas kernels for 19% -> 20%
where the time goes in v4:
time: 58.6 us; the launch traced here: 58.2 us
  starting transfers between devices  29.4 us (50%)
  Pallas kernels  19.2 us (33%)
  waiting for transfers between devices  9.31 us (16%)
    ppermute x4, starting transfers between devices, routed(): return lax.ppermute(value, axis, route)  19.2 us
    all_to_all x1, starting transfers between devices, body(): lax.all_to_all(sent, 'yz', split_axis=0, concat_axis=0, tiled=True)  10.2 us
    pallas_call x1, Pallas kernels, ready_call(): pl.pallas_call(ready_kernel, name='ready', out_shape=(jax.ShapeDtypeStruc...  9.39 us
    all_to_all x1, waiting for transfers between devices, body(): lax.all_to_all(sent, 'yz', split_axis=0, concat_axis=0, tiled=True)  6.65 us
    pallas_call x1, Pallas kernels, final_call(): pl.pallas_call(final_kernel, name='final', out_shape=jax.ShapeDtypeStruct...  4.44 us
    ppermute x4, waiting for transfers between devices, routed(): return lax.ppermute(value, axis, route)  2.66 us
    pallas_call x1, Pallas kernels, coarse_call(): pl.pallas_call(coarse_kernel, name='coarse', out_shape=(jax.ShapeDtypeStr...  2.44 us
    pallas_call x1, Pallas kernels, payload_call(): pl.pallas_call(payload_kernel, name='payload', out_shape=jax.ShapeDtypeSt...  1.96 us
  transfers between devices with their start and end apart: 5, of which 2 were waited for; matrix products, arithmetic and copies ran while one was open for 0% of the time, Pallas kernels for 20%

profile of v4, /device:TPU:1, one launch (start us, length us, event | category | flops | bytes accessed | tf_op | source)
XLA Modules:
  0.0 58.2 jit_solution(16051429839999067852)
XLA Ops:
  0.0 2.0 %payload.1 = bf16[16,136,128]{2,1,0:T(8,128)(2,1)} custom-call(bf16[64,256]{1,0:T(8,128)(2,1)} %bitcast.8, s32[8,8]{1,0:T(8,128)} %parent_ref.1, s32[8,8]{1,0:T(8,128)} %octant_ref.1, s32[8,8]{1,0:T(8,128)} %bitcast.12, s32[8,8]{1,0:T(8,128)} %bitcast.13), custom_call_target="tpu_custom_call" | custom-call | flops 1000000000 | bytes 1048576 | tf_op jit(solution)/shard_map/payload/pallas_call | solution.py:399
  2.0 10.2 %all-to-all-start = ((bf16[16,136,128]{2,1,0:T(8,128)(2,1)}), bf16[16,136,128]{2,1,0:T(8,128)(2,1)S(1)}, u32[]{:S(2)}, u32[]{:S(2)}) async-start(bf16[16,136,128]{2,1,0:T(8,128)(2,1)} %payload.1), calls=%async_computation | async-start | bytes 1114112 | tf_op jit(solution)/shard_map/all_to_all | solution.py:504
  12.2 0.0 copy-start.1
  12.2 9.4 %ready.1 = (f32[16,128,128]{2,1,0:T(8,128)}, bf16[3,1024,192]{2,1,0:T(8,128)(2,1)}, bf16[128,256]{1,0:T(8,128)(2,1)}, bf16[256,2048]{1,0:T(8,128)(2,1)}, bf16[256,2048]{1,0:T(8,128)(2,1)}) custom-call(s32[1]{0:T(128)} %bitcast.parity_ref, s32[16,16]{1,0:T(8,128)} %src_ref.1, s32[16,16]{1,0:T(8,128)} %kind_ref.1, s32[16]{0:T(128)} %count_ref.1, ...), custom_call_target="tpu_custom_call" | custom-call | flops 8000000000 | bytes 6291456 | tf_op jit(solution)/shard_map/ready/pallas_call | solution.py:378
  21.6 6.7 %all-to-all-done.gathered_ref = bf16[16,136,128]{2,1,0:T(8,128)(2,1)S(1)} async-done(((bf16[16,136,128]{2,1,0:T(8,128)(2,1)}), bf16[16,136,128]{2,1,0:T(8,128)(2,1)S(1)}, u32[]{:S(2)}, u32[]{:S(2)}) %all-to-all-start) | async-done | bytes 557088 | tf_op jit(solution)/shard_map/all_to_all | solution.py:504
  28.3 0.0 copy-done.1
  28.3 0.0 copy-start.2
  28.3 0.0 copy-start.4
  28.3 1.0 %parents.1 = (bf16[320,256]{1,0:T(8,128)(2,1)S(1)}, bf16[128,256]{1,0:T(8,128)(2,1)S(1)}) custom-call(s32[1]{0:T(128)} %bitcast.7.own_ref, bf16[16,136,128]{2,1,0:T(8,128)(2,1)S(1)} %all-to-all-done.gathered_ref, bf16[8,256,256]{2,1,0:T(8,128)(2,1)S(1)} %copy-done.1), custom_call_target="tpu_custom_call" | custom-call | flops 2000000000 | bytes 2097152 | tf_op jit(solution)/shard_map/parents/pallas_call | solution.py:419
  29.3 6.6 %collective-permute-start.1 = (bf16[320,256]{1,0:T(8,128)(2,1)S(1)}, bf16[320,256]{1,0:T(8,128)(2,1)S(1)}, u32[]{:S(2)}, u32[]{:S(2)}) collective-permute-start(bf16[320,256]{1,0:T(8,128)(2,1)S(1)} %get-tuple-element.16.own_ref), channel_id=1, source_target_pairs={{0,496},{16,32},{32,16},{48,64},{64,48},{80,96},{96,80},{112,128},... | collective-permute-start | bytes 491528 | tf_op jit(solution)/shard_map/ppermute | solution.py:473
  35.9 6.4 %collective-permute-start.2 = (bf16[320,256]{1,0:T(8,128)(2,1)S(1)}, bf16[320,256]{1,0:T(8,128)(2,1)S(1)}, u32[]{:S(2)}, u32[]{:S(2)}) collective-permute-start(bf16[320,256]{1,0:T(8,128)(2,1)S(1)} %get-tuple-element.16.own_ref), channel_id=1, source_target_pairs={{0,16},{16,0},{32,48},{48,32},{64,80},{80,64},{96,112},{112,96},{1... | collective-permute-start | bytes 491528 | tf_op jit(solution)/shard_map/ppermute | solution.py:473
  42.3 4.2 %collective-permute-start = (bf16[128,256]{1,0:T(8,128)(2,1)S(1)}, bf16[128,256]{1,0:T(8,128)(2,1)S(1)}, u32[]{:S(2)}, u32[]{:S(2)}) collective-permute-start(bf16[128,256]{1,0:T(8,128)(2,1)S(1)} %get-tuple-element.20), channel_id=1, source_target_pairs={{0,32},{16,496},{32,64},{48,16},{64,96},{80,48},{96,128},{112,80},... | collective-permute-start | bytes 196616 | tf_op jit(solution)/shard_map/ppermute | solution.py:473
  46.5 1.9 %collective-permute-start.3 = (bf16[128,256]{1,0:T(8,128)(2,1)S(1)}, bf16[128,256]{1,0:T(8,128)(2,1)S(1)}, u32[]{:S(2)}, u32[]{:S(2)}) collective-permute-start(bf16[128,256]{1,0:T(8,128)(2,1)S(1)} %get-tuple-element.20), channel_id=1, source_target_pairs={{0,480},{16,48},{32,0},{48,80},{64,32},{80,112},{96,64},{112,144},... | collective-permute-start | bytes 196616 | tf_op jit(solution)/shard_map/ppermute | solution.py:473
  48.5 0.0 copy-done.2
  48.5 0.0 copy-done.4
  48.5 0.0 copy-start
  48.5 0.0 copy-start.3
  48.5 0.0 copy-start.5
  48.5 0.0 copy-start.6
  48.5 0.0 copy-start.7
  48.5 0.0 copy-start.8
  48.6 2.4 %coarse.1 = (f32[1024,256]{1,0:T(8,128)S(1)}, f32[1024,256]{1,0:T(8,128)S(1)}, bf16[1024,512]{1,0:T(8,128)(2,1)S(1)}) custom-call(s32[1]{0:T(128)} %bitcast.parity_ref, s32[8,8]{1,0:T(8,128)S(1)} %copy-done.2, bf16[16,136,128]{2,1,0:T(8,128)(2,1)S(1)} %all-to-all-done.gathered_ref, bf16[320,256]{1,0:T(8,128)(2,1)S(1)} %get-tuple-element.16.own_ref, ...), custom_call_target="tpu_custom_call" | custom-call | flops 3000000000 | bytes 4194304 | tf_op jit(solution)/shard_map/coarse/pallas_call | solution.py:437
  51.0 0.0 collective-permute-done.near2_ref
  51.0 2.7 %collective-permute-done.3.far2_ref = bf16[128,256]{1,0:T(8,128)(2,1)S(1)} collective-permute-done((bf16[128,256]{1,0:T(8,128)(2,1)S(1)}, bf16[128,256]{1,0:T(8,128)(2,1)S(1)}, u32[]{:S(2)}, u32[]{:S(2)}) %collective-permute-start.3) | collective-permute-done | bytes 65568 | tf_op jit(solution)/shard_map/ppermute | solution.py:473
  53.7 0.0 collective-permute-done.1.near1_ref
  53.7 0.0 collective-permute-done.2.mate_ref
  53.7 0.0 copy-done
  53.7 0.0 copy-done.3
  53.7 0.0 copy-done.5
  53.7 0.0 copy-done.6
  53.7 0.0 copy-done.7
  53.7 0.0 copy-done.8
  53.7 4.4 %final.1 = bf16[16,128,128]{2,1,0:T(8,128)(2,1)} custom-call(s32[8,8]{1,0:T(8,128)S(1)} %copy-done.3, bf16[3,1024,192]{2,1,0:T(8,128)(2,1)S(1)} %copy-done.4, f32[1024,256]{1,0:T(8,128)S(1)} %get-tuple-element.17.leaf_ref, f32[1024,256]{1,0:T(8,128)S(1)} %get-tuple-element.18.coarse_ref, bf16[1024,512]{1,0:T(8,128)(2,1)S(1)} %get-tuple-element.19.coarse_counts_ref, ...), custom_call_target="tpu_custom_call" | custom-call | flops 4000000000 | bytes 8388608 | tf_op jit(solution)/shard_map/final/pallas_call | solution.py:456
Async XLA Ops:
  2.0 26.3 %all-to-all-start = ((bf16[16,136,128]{2,1,0:T(8,128)(2,1)}), bf16[16,136,128]{2,1,0:T(8,128)(2,1)S(1)}, u32[]{:S(2)}, u32[]{:S(2)}) async-start(bf16[16,136,128]{2,1,0:T(8,128)(2,1)} %payload.1), calls=%async_computation | async-start | bytes 1114112 | tf_op jit(solution)/shard_map/all_to_all | solution.py:504
  12.2 16.1 %copy-start.1 = (bf16[8,256,256]{2,1,0:T(8,128)(2,1)S(1)}, bf16[8,256,256]{2,1,0:T(8,128)(2,1)}, u32[]{:S(2)}) copy-start(bf16[8,256,256]{2,1,0:T(8,128)(2,1)} %shift_ref.3) | copy-start | bytes 3145732
  28.3 20.2 %copy-start.2 = (s32[8,8]{1,0:T(8,128)S(1)}, s32[8,8]{1,0:T(8,128)}, u32[]{:S(2)}) copy-start(s32[8,8]{1,0:T(8,128)} %parent_ref.1) | copy-start | bytes 772
  28.3 20.2 %copy-start.4 = (bf16[3,1024,192]{2,1,0:T(8,128)(2,1)S(1)}, bf16[3,1024,192]{2,1,0:T(8,128)(2,1)}, u32[]{:S(2)}) copy-start(bf16[3,1024,192]{2,1,0:T(8,128)(2,1)} %get-tuple-element.15.counts_ref) | copy-start | bytes 3538948
  29.3 24.4 %collective-permute-start.1 = (bf16[320,256]{1,0:T(8,128)(2,1)S(1)}, bf16[320,256]{1,0:T(8,128)(2,1)S(1)}, u32[]{:S(2)}, u32[]{:S(2)}) collective-permute-start(bf16[320,256]{1,0:T(8,128)(2,1)S(1)} %get-tuple-element.16.own_ref), channel_id=1, source_target_pairs={{0,496},{16,32},{32,16},{48,64},{64,48},{80,96},{96,80},{112,128},... | collective-permute-start | bytes 491528 | tf_op jit(solution)/shard_map/ppermute | solution.py:473
  35.9 17.8 %collective-permute-start.2 = (bf16[320,256]{1,0:T(8,128)(2,1)S(1)}, bf16[320,256]{1,0:T(8,128)(2,1)S(1)}, u32[]{:S(2)}, u32[]{:S(2)}) collective-permute-start(bf16[320,256]{1,0:T(8,128)(2,1)S(1)} %get-tuple-element.16.own_ref), channel_id=1, source_target_pairs={{0,16},{16,0},{32,48},{48,32},{64,80},{80,64},{96,112},{112,96},{1... | collective-permute-start | bytes 491528 | tf_op jit(solution)/shard_map/ppermute | solution.py:473
  42.3 8.7 %collective-permute-start = (bf16[128,256]{1,0:T(8,128)(2,1)S(1)}, bf16[128,256]{1,0:T(8,128)(2,1)S(1)}, u32[]{:S(2)}, u32[]{:S(2)}) collective-permute-start(bf16[128,256]{1,0:T(8,128)(2,1)S(1)} %get-tuple-element.20), channel_id=1, source_target_pairs={{0,32},{16,496},{32,64},{48,16},{64,96},{80,48},{96,128},{112,80},... | collective-permute-start | bytes 196616 | tf_op jit(solution)/shard_map/ppermute | solution.py:473
  46.5 7.1 %collective-permute-start.3 = (bf16[128,256]{1,0:T(8,128)(2,1)S(1)}, bf16[128,256]{1,0:T(8,128)(2,1)S(1)}, u32[]{:S(2)}, u32[]{:S(2)}) collective-permute-start(bf16[128,256]{1,0:T(8,128)(2,1)S(1)} %get-tuple-element.20), channel_id=1, source_target_pairs={{0,480},{16,48},{32,0},{48,80},{64,32},{80,112},{96,64},{112,144},... | collective-permute-start | bytes 196616 | tf_op jit(solution)/shard_map/ppermute | solution.py:473
  48.5 5.2 %copy-start = (bf16[16,256,256]{2,1,0:T(8,128)(2,1)S(1)}, bf16[16,256,256]{2,1,0:T(8,128)(2,1)}, u32[]{:S(2)}) copy-start(bf16[16,256,256]{2,1,0:T(8,128)(2,1)} %operators_ref.1) | copy-start | bytes 6291460
  48.5 5.2 %copy-start.3 = (s32[8,8]{1,0:T(8,128)S(1)}, s32[8,8]{1,0:T(8,128)}, u32[]{:S(2)}) copy-start(s32[8,8]{1,0:T(8,128)} %octant_ref.1) | copy-start | bytes 772
  48.5 5.2 %copy-start.5 = (f32[16,128,128]{2,1,0:T(8,128)S(1)}, f32[16,128,128]{2,1,0:T(8,128)}, u32[]{:S(2)}) copy-start(f32[16,128,128]{2,1,0:T(8,128)} %get-tuple-element.24.near_ref) | copy-start | bytes 3145732
  48.5 5.2 %copy-start.6 = (bf16[256,2048]{1,0:T(8,128)(2,1)S(1)}, bf16[256,2048]{1,0:T(8,128)(2,1)}, u32[]{:S(2)}) copy-start(bf16[256,2048]{1,0:T(8,128)(2,1)} %get-tuple-element.22.right_high_ref) | copy-start | bytes 3145732
  48.5 5.2 %copy-start.7 = (bf16[256,2048]{1,0:T(8,128)(2,1)S(1)}, bf16[256,2048]{1,0:T(8,128)(2,1)}, u32[]{:S(2)}) copy-start(bf16[256,2048]{1,0:T(8,128)(2,1)} %get-tuple-element.23.right_low_ref) | copy-start | bytes 3145732
  48.5 5.2 %copy-start.8 = (bf16[128,256]{1,0:T(8,128)(2,1)S(1)}, bf16[128,256]{1,0:T(8,128)(2,1)}, u32[]{:S(2)}) copy-start(bf16[128,256]{1,0:T(8,128)(2,1)} %get-tuple-element.21.left_ref) | copy-start | bytes 196612
